TPU v7x, 32 devices: a whole 2x2x4 slice. The times are simulated.
32 devices in a mesh: dp: 4 (over y, x), fsdp: 8 (over z, core).
Axes of the slice: x: 2, y: 2, z: 4, core: 2. Of those that a mesh axis runs over, the one named last changes fastest.
Arguments:
- tokens: bfloat16 [32, 1024, 768], P(('dp', 'fsdp')), may hold values from -6 to 6
- lengths: int32 [32], P(('dp', 'fsdp')), may hold values from 256 to 1024, as said below
- cells: int32 [32, 1024], P(('dp', 'fsdp')), may hold values 0 or 1
- cotangent: bfloat16 [32, 1024, 768], P(('dp', 'fsdp')), may hold values from -6 to 6
- ln1_gain: bfloat16 [768], P('fsdp'), may hold values from 0.5 to 1.5
- ln1_bias: bfloat16 [768], P('fsdp'), may hold values from -3 to 3
- w_qkv: bfloat16 [768, 2304], P('fsdp'), may hold values from -0.21875 to 0.21875
- b_query: bfloat16 [768], P('fsdp'), may hold values from -6 to 6
- b_value: bfloat16 [768], P('fsdp'), may hold values from -6 to 6
- w_out: bfloat16 [768, 768], P('fsdp'), may hold values from -0.875 to 0.875
- b_out: bfloat16 [768], P('fsdp'), may hold values from -3 to 3
- ln2_gain: bfloat16 [768], P('fsdp'), may hold values from 0.5 to 1.5
- ln2_bias: bfloat16 [768], P('fsdp'), may hold values from -3 to 3
- w_up: bfloat16 [768, 3072], P('fsdp'), may hold values from -0.21875 to 0.21875
- b_up: bfloat16 [3072], P('fsdp'), may hold values from -3 to 3
- w_down: bfloat16 [3072, 768], P('fsdp'), may hold values from -0.109375 to 0.109375
- b_down: bfloat16 [768], P('fsdp'), may hold values from -3 to 3
Outputs:
- output: bfloat16 [32, 1024, 768], P(('dp', 'fsdp'))
- grad_tokens: float32 [32, 1024, 768], P(('dp', 'fsdp'))
- grad_ln1_gain: float32 [768], P('fsdp')
- grad_ln1_bias: float32 [768], P('fsdp')
- grad_w_qkv: float32 [768, 2304], P('fsdp')
- grad_b_query: float32 [768], P('fsdp')
- grad_b_value: float32 [768], P('fsdp')
- grad_w_out: float32 [768, 768], P('fsdp')
- grad_b_out: float32 [768], P('fsdp')
- grad_ln2_gain: float32 [768], P('fsdp')
- grad_ln2_bias: float32 [768], P('fsdp')
- grad_w_up: float32 [768, 3072], P('fsdp')
- grad_b_up: float32 [3072], P('fsdp')
- grad_w_down: float32 [3072, 768], P('fsdp')
- grad_b_down: float32 [768], P('fsdp')
Inputs may be any that keep to these rules, and one draw needn't show every extreme that they name: `lengths`: each sequence has at least 256 valid tokens, and some sequence fills all 1024 slots.
All inputs are finite; a program needn't handle non-finite values. No bound on the sum of `cells` on one device may be relied on, other than what follows from the above.
Results may differ from a plain program's by a relative error of at most 0.019.
Values may be sent and summed in bfloat16 or wider, within the bound.
A program may use at most 128 MiB of HBM per device.

v0:
```python
from functools import partial
import math

import jax
import jax.numpy as jnp
from jax import lax
from jax.experimental import pallas as pl
from jax.experimental.pallas import tpu as pltpu
from jax.sharding import PartitionSpec as P

HEADS = 12
EPSILON = 1e-05
GELU_C = 0.7978845608028654
GELU_A = 0.044715
MASKED = -1e30
TILE = 256
VMEM_BYTES = 60 * 1024 * 1024
F32 = jnp.float32
BF16 = jnp.bfloat16


def mm(a, b):
    return jnp.dot(a, b, preferred_element_type=F32)


def mm_nt(a, b):
    return lax.dot_general(a, b, (((1,), (1,)), ((), ())), preferred_element_type=F32)


def mm_tn(a, b):
    return lax.dot_general(a, b, (((0,), (0,)), ((), ())), preferred_element_type=F32)


def params(**kw):
    return pltpu.CompilerParams(
        dimension_semantics=("arbitrary",), vmem_limit_bytes=VMEM_BYTES, **kw
    )


def cost(flops, bytes_accessed, transcendentals=0):
    return pl.CostEstimate(
        flops=int(flops), bytes_accessed=int(bytes_accessed), transcendentals=int(transcendentals)
    )


def norm_forward(values):
    row_mean = jnp.mean(values, axis=-1, keepdims=True)
    centered = values - row_mean
    inv_std = lax.rsqrt(jnp.mean(centered * centered, axis=-1, keepdims=True) + EPSILON)
    return centered * inv_std, inv_std


def norm_backward(grad_normed, normalized, inv_std, gain):
    scaled = grad_normed * gain
    return inv_std * (
        scaled
        - jnp.mean(scaled, axis=-1, keepdims=True)
        - normalized * jnp.mean(scaled * normalized, axis=-1, keepdims=True)
    )


def gelu_pair(u):
    square = u * u
    tanh_part = jnp.tanh(u * (GELU_C + (GELU_C * GELU_A) * square))
    half = 0.5 + 0.5 * tanh_part
    value = u * half
    slope = half + value * (1.0 - tanh_part) * (GELU_C + (3.0 * GELU_C * GELU_A) * square)
    return value, slope


def whole(shape):
    return pl.BlockSpec(shape, lambda i: (0,) * len(shape), pipeline_mode=pl.Buffered(1))


def rows_spec(tile, width):
    return pl.BlockSpec((tile, width), lambda i: (i, 0))


def qkv_kernel(scale, x_ref, w_ref, vec_ref, a1_ref, qkv_ref):
    width = x_ref.shape[1]
    gain, shift, bq, bv = (vec_ref[i : i + 1, :] for i in range(4))
    xhat, _ = norm_forward(x_ref[...].astype(F32))
    a1 = (xhat * gain + shift).astype(BF16)
    a1_ref[...] = a1
    q = mm(a1, w_ref[0])
    qkv_ref[:, 0:width] = ((q + bq) * scale).astype(BF16)
    k = mm(a1, w_ref[1])
    qkv_ref[:, width : 2 * width] = k.astype(BF16)
    v = mm(a1, w_ref[2])
    qkv_ref[:, 2 * width : 3 * width] = (v + bv).astype(BF16)


def qkv_forward(x, ab, vecs, scale):
    rows, width = x.shape
    return pl.pallas_call(
        partial(qkv_kernel, scale),
        grid=(rows // TILE,),
        in_specs=[rows_spec(TILE, width), whole((3, width, width)), whole(vecs.shape)],
        out_specs=[rows_spec(TILE, width), rows_spec(TILE, 3 * width)],
        out_shape=[
            jax.ShapeDtypeStruct((rows, width), BF16),
            jax.ShapeDtypeStruct((rows, 3 * width), BF16),
        ],
        compiler_params=params(),
        cost_estimate=cost(6 * rows * width * width, 12 * rows * width),
        name="qkv_forward",
    )(x, ab, vecs)


def split3(value):
    first = value.astype(BF16)
    rest = value - first.astype(F32)
    second = rest.astype(BF16)
    third = (rest - second.astype(F32)).astype(BF16)
    return first, second, third


def attn_fwd_kernel(q_ref, k_ref, v_ref, kbias_ref, rbias_ref, o_ref, qa_ref, mask_ref):
    blocks = q_ref.shape[0] // TILE
    lane = lax.broadcasted_iota(jnp.int32, (1, 128), 1)

    @pl.when(pl.program_id(0) == 0)
    def _():
        row = lax.broadcasted_iota(jnp.int32, (TILE, TILE), 0)
        col = lax.broadcasted_iota(jnp.int32, (TILE, TILE), 1)
        for i in range(blocks):
            usable = rbias_ref[:, i * TILE : (i + 1) * TILE]
            mask_ref[i] = jnp.where(row == col, 0.0, jnp.where(row > col, usable, MASKED))

    zero = jnp.zeros((), BF16)
    one = jnp.ones((), BF16)
    for head in range(2):
        base = 64 * head
        extra = 64 - base
        own = (lane >= base) & (lane < base + 64)
        k_off = jnp.where(own, k_ref[...], jnp.where(lane == extra, kbias_ref[...], zero))
        for i in range(blocks):
            here = slice(i * TILE, (i + 1) * TILE)
            q = jnp.where(own, q_ref[here, :], zero)
            q_off = jnp.where(lane == extra, one, q)
            s_diag = mm_nt(q, k_ref[here, :]) + mask_ref[i]
            row_max = jnp.max(s_diag, axis=-1, keepdims=True)
            if i:
                s_off = mm_nt(q_off, k_off[: i * TILE])
                row_max = jnp.maximum(row_max, jnp.max(s_off, axis=-1, keepdims=True))
            e_diag = jnp.exp(s_diag - row_max)
            total = jnp.sum(e_diag, axis=-1, keepdims=True)
            o = mm(e_diag.astype(BF16), v_ref[here, :])
            if i:
                e_off = jnp.exp(s_off - row_max)
                total += jnp.sum(e_off, axis=-1, keepdims=True)
                o += mm(e_off.astype(BF16), v_ref[0 : i * TILE, :])
            o = (o * (1.0 / total)).astype(BF16)
            if head:
                o_ref[here, :] = jnp.where(own, o, o_ref[here, :])
            else:
                o_ref[here, :] = o
            first, second, third = split3(-(row_max + jnp.log(total)))
            qa = jnp.where(lane == extra + 1, first, q_off)
            qa = jnp.where(lane == extra + 2, second, qa)
            qa = jnp.where(lane == extra + 3, third, qa)
            qa_ref[here, 128 * head : 128 * head + 128] = qa


def attn_forward(qkv, kbias, rbias):
    rows = qkv.shape[0]
    width = qkv.shape[1] // 3
    pairs = width // 128

    def part(p):
        return pl.BlockSpec((rows, 128), lambda i: (0, p * pairs + i))

    return pl.pallas_call(
        attn_fwd_kernel,
        grid=(pairs,),
        in_specs=[part(0), part(1), part(2), whole(kbias.shape), whole(rbias.shape)],
        out_specs=[part(0), pl.BlockSpec((rows, 256), lambda i: (0, i))],
        out_shape=[
            jax.ShapeDtypeStruct((rows, width), BF16),
            jax.ShapeDtypeStruct((rows, 2 * width), BF16),
        ],
        scratch_shapes=[pltpu.VMEM((rows // TILE, TILE, TILE), F32)],
        compiler_params=params(),
        cost_estimate=cost(8 * rows * rows * width, 12 * rows * width),
        name="attn_forward",
    )(qkv, qkv, qkv, kbias, rbias)


def attn_bwd_kernel(
    qa_ref, k_ref, v_ref, o_ref, do_ref, kbias_ref, dq_ref, dk_ref, dv_ref, mask_ref, doa_ref, dqt_ref,
    between=None,
):
    rows = k_ref.shape[0]
    blocks = rows // TILE
    lane = lax.broadcasted_iota(jnp.int32, (1, 128), 1)

    @pl.when(pl.program_id(0) == 0)
    def _():
        key = lax.broadcasted_iota(jnp.int32, (TILE, TILE), 0)
        query = lax.broadcasted_iota(jnp.int32, (TILE, TILE), 1)
        for i in range(blocks):
            usable = kbias_ref[i * TILE : (i + 1) * TILE, 0:1].astype(F32)
            mask_ref[i] = jnp.where(key == query, 0.0, jnp.where(query > key, usable, MASKED))

    zero = jnp.zeros((), BF16)
    one = jnp.ones((), BF16)
    product = do_ref[...].astype(F32) * o_ref[...].astype(F32)
    kt = k_ref[...].T
    for head in range(2):
        base = 64 * head
        extra = 64 - base
        own = (lane >= base) & (lane < base + 64)
        terms = (lane > extra) & (lane <= extra + 3)
        qa_cols = slice(128 * head, 128 * head + 128)
        if between is not None:
            between(head)
        inner = -jnp.sum(jnp.where(own, product, 0.0), axis=-1, keepdims=True)
        first, second, third = split3(inner)
        doa = jnp.where(own, do_ref[...], zero)
        doa = jnp.where(lane == extra + 1, first, doa)
        doa = jnp.where(lane == extra + 2, second, doa)
        doa_ref[...] = jnp.where(lane == extra + 3, third, doa)
        for j in range(blocks):
            here = slice(j * TILE, (j + 1) * TILE)
            after = slice((j + 1) * TILE, rows)
            k_diag = jnp.where(own, k_ref[here, :], jnp.where(terms, one, zero))
            v_aug = jnp.where(own, v_ref[here, :], jnp.where(terms, one, zero))
            p_diag = jnp.exp(mm_nt(k_diag, qa_ref[here, qa_cols]) + mask_ref[j])
            dp_diag = mm_nt(v_aug, doa_ref[here, :])
            ds_diag = (p_diag * dp_diag).astype(BF16)
            dv = mm(p_diag.astype(BF16), do_ref[here, :])
            dk = mm(ds_diag, qa_ref[here, qa_cols])
            dq_diag = mm(kt[:, here], ds_diag)
            if j:
                dqt_ref[:, here] += dq_diag
            else:
                dqt_ref[:, here] = dq_diag
            if j + 1 < blocks:
                k_off = jnp.where(lane == extra, kbias_ref[here, :], k_diag)
                p_off = jnp.exp(mm_nt(k_off, qa_ref[after, qa_cols]))
                dp_off = mm_nt(v_aug, doa_ref[after, :])
                ds_off = (p_off * dp_off).astype(BF16)
                dv += mm(p_off.astype(BF16), do_ref[after, :])
                dk += mm(ds_off, qa_ref[after, qa_cols])
                dq_off = mm(kt[:, here], ds_off)
                if j:
                    dqt_ref[:, after] += dq_off
                else:
                    dqt_ref[:, after] = dq_off
            dk = dk.astype(BF16)
            dv = dv.astype(BF16)
            if head:
                dk_ref[here, :] = jnp.where(own, dk, dk_ref[here, :])
                dv_ref[here, :] = jnp.where(own, dv, dv_ref[here, :])
            else:
                dk_ref[here, :] = dk
                dv_ref[here, :] = dv
        dq = (dqt_ref[...] * 0.125).astype(BF16).T
        if head:
            dq_ref[...] = jnp.where(own, dq, dq_ref[...])
        else:
            dq_ref[...] = dq


def attn_backward(qa, qkv, o, do, kbias, first_pair, pair_count):
    rows, width = o.shape
    pairs = width // 128

    def part(p):
        return pl.BlockSpec((rows, 128), lambda i: (0, p * pairs + first_pair + i))

    out = pl.BlockSpec((rows, 128), lambda i: (0, i))
    shape = jax.ShapeDtypeStruct((rows, 128 * pair_count), BF16)
    return pl.pallas_call(
        attn_bwd_kernel,
        grid=(pair_count,),
        in_specs=[
            pl.BlockSpec((rows, 256), lambda i: (0, first_pair + i)),
            part(1),
            part(2),
            part(0),
            part(0),
            whole(kbias.shape),
        ],
        out_specs=[out, out, out],
        out_shape=[shape, shape, shape],
        scratch_shapes=[
            pltpu.VMEM((rows // TILE, TILE, TILE), F32),
            pltpu.VMEM((rows, 128), BF16),
            pltpu.VMEM((128, rows), F32),
        ],
        compiler_params=params(),
        cost_estimate=cost(20 * rows * rows * 128 * pair_count, 18 * rows * 128 * pair_count),
        name="attn_backward",
    )(qa, qkv, qkv, o, do, kbias)


def mlp_kernel(
    x_ref, o_ref, cot_ref, valid_ref, wo_ref, wu_ref, wd_ref, vec_ref, bu_ref,
    out_ref, dm_ref, a2_ref, g_ref, du_ref, dr_ref, dy_ref, do_ref,
    s_gain_ref, s_shift_ref, s_bu_ref, s_bd_ref, s_bo_ref,
):
    chunk = wu_ref.shape[2]
    hidden = wd_ref.shape[0]
    bo, gain, shift, bd = (vec_ref[i : i + 1, :] for i in range(4, 8))
    middle = x_ref[...].astype(F32) + mm(o_ref[...], wo_ref[0]) + bo
    xhat, inv_std = norm_forward(middle)
    a2 = (xhat * gain + shift).astype(BF16)
    a2_ref[...] = a2
    dout = cot_ref[...].astype(F32) * valid_ref[:, 0:1]
    dm = dout.astype(BF16)
    dm_ref[...] = dm
    out = middle + bd
    da2 = jnp.zeros_like(middle)
    first = pl.program_id(0) == 0

    def add_sum(ref, cols, value):
        part = jnp.sum(value, axis=0, keepdims=True)
        ref[:, cols] = jnp.where(first, part, ref[:, cols] + part)

    for c in range(hidden // chunk):
        cols = slice(c * chunk, (c + 1) * chunk)
        u = mm(a2, wu_ref[c]) + bu_ref[:, cols]
        value, slope = gelu_pair(u)
        g = value.astype(BF16)
        g_ref[:, cols] = g
        out += mm(g, wd_ref[cols, :])
        du = (mm_nt(dm, wd_ref[cols, :]) * slope).astype(BF16)
        du_ref[:, cols] = du
        add_sum(s_bu_ref, cols, du.astype(F32))
        da2 += mm_nt(du, wu_ref[c])
    out_ref[...] = out.astype(BF16)
    every = slice(None)
    add_sum(s_bd_ref, every, dm.astype(F32))
    add_sum(s_gain_ref, every, da2 * xhat)
    add_sum(s_shift_ref, every, da2)
    dr = dout + norm_backward(da2, xhat, inv_std, gain)
    dr_ref[...] = dr
    dy = dr.astype(BF16)
    dy_ref[...] = dy
    add_sum(s_bo_ref, every, dy.astype(F32))
    do_ref[...] = mm_nt(dy, wo_ref[0]).astype(BF16)


def mlp_both(x, o, cot, valid, ab, w_down, vecs, b_up):
    rows, width = x.shape
    hidden = w_down.shape[0]
    row = rows_spec(TILE, width)
    wide = rows_spec(TILE, hidden)
    acc = pl.BlockSpec((1, width), lambda i: (0, 0))
    acc_wide = pl.BlockSpec((1, hidden), lambda i: (0, 0))

    def shape(r, c, t):
        return jax.ShapeDtypeStruct((r, c), t)

    return pl.pallas_call(
        mlp_kernel,
        grid=(rows // TILE,),
        in_specs=[
            row, row, row, rows_spec(TILE, 128),
            pl.BlockSpec((1, width, width), lambda i: (3, 0, 0), pipeline_mode=pl.Buffered(1)),
            pl.BlockSpec((4, width, width), lambda i: (1, 0, 0), pipeline_mode=pl.Buffered(1)),
            whole(w_down.shape), whole(vecs.shape), whole(b_up.shape),
        ],
        out_specs=[row, row, row, wide, wide, row, row, row, acc, acc, acc_wide, acc, acc],
        out_shape=[
            shape(rows, width, BF16), shape(rows, width, BF16), shape(rows, width, BF16),
            shape(rows, hidden, BF16), shape(rows, hidden, BF16), shape(rows, width, F32),
            shape(rows, width, BF16), shape(rows, width, BF16),
            shape(1, width, F32), shape(1, width, F32), shape(1, hidden, F32),
            shape(1, width, F32), shape(1, width, F32),
        ],
        compiler_params=params(),
        cost_estimate=cost(rows * width * (8 * hidden + 4 * width), 24 * rows * width + 12 * rows * hidden),
        name="mlp_both",
    )(x, o, cot, valid, ab, ab, w_down, vecs, b_up)


def input_kernel(
    x_ref, dq_ref, dk_ref, dv_ref, dr_ref, w_ref, vec_ref, out_ref, s_gain_ref, s_shift_ref, s_bq_ref, s_bv_ref
):
    width = x_ref.shape[1]
    xhat, inv_std = norm_forward(x_ref[...].astype(F32))
    da = mm_nt(dq_ref[...], w_ref[0])
    da += mm_nt(dk_ref[...], w_ref[1])
    da += mm_nt(dv_ref[...], w_ref[2])
    first = pl.program_id(0) == 0

    def add_sum(ref, value):
        part = jnp.sum(value, axis=0, keepdims=True)
        ref[...] = jnp.where(first, part, ref[...] + part)

    add_sum(s_gain_ref, da * xhat)
    add_sum(s_shift_ref, da)
    add_sum(s_bq_ref, dq_ref[...].astype(F32))
    add_sum(s_bv_ref, dv_ref[...].astype(F32))
    out_ref[...] = dr_ref[...] + norm_backward(da, xhat, inv_std, vec_ref[0:1, :])


def input_grad(x, dq, dk, dv, dr, ab, vecs):
    rows, width = x.shape
    row = rows_spec(TILE, width)
    acc = pl.BlockSpec((1, width), lambda i: (0, 0))
    vec = jax.ShapeDtypeStruct((1, width), F32)
    return pl.pallas_call(
        input_kernel,
        grid=(rows // TILE,),
        in_specs=[row, row, row, row, row, whole((3, width, width)), whole(vecs.shape)],
        out_specs=[row, acc, acc, acc, acc],
        out_shape=[jax.ShapeDtypeStruct((rows, width), F32), vec, vec, vec, vec],
        compiler_params=params(),
        cost_estimate=cost(6 * rows * width * width, 16 * rows * width),
        name="input_grad",
    )(x, dq, dk, dv, dr, ab, vecs)


def mask_terms(lengths, cells, context):
    usable = (jnp.arange(context) < lengths[0]) & (cells[0] == 1)
    bias = jnp.where(usable, 0.0, MASKED)
    kbias = jnp.broadcast_to(bias.astype(BF16)[:, None], (context, 128))
    rbias = bias[None, :]
    valid = jnp.broadcast_to(
        (jnp.arange(context) < lengths[0]).astype(F32)[:, None], (context, 128)
    )
    return kbias, rbias, valid


def gather_kernel(nz, n_small, own_ref, small_ref, ab_ref, c_ref, all_small_ref, send, recv, local):
    d = lax.axis_index("dp")
    f = lax.axis_index("fsdp")
    z, c = f // 2, f % 2
    half = own_ref.shape[2] // 2
    mate = z * 2 + (1 - c)
    flip_x = d + 1 - 2 * (d % 2)
    flip_y = lax.rem(d + 2, 4)
    flip_xy = lax.rem(flip_x + 2, 4)
    others = [lax.rem(z + k, nz) for k in range(1, nz)]

    barrier = pltpu.get_barrier_semaphore()
    partners = [(flip_x, f), (flip_y, f), (d, mate)]
    for o in others:
        partners += [(d, o * 2 + c), (d, o * 2 + 1 - c)]
    for p in partners:
        pl.semaphore_signal(barrier, inc=1, device_id=p, device_id_type=pl.DeviceIdType.MESH)
    pl.semaphore_wait(barrier, len(partners))

    def slot(g, block, shard):
        if g == 2:
            return c_ref.at[shard, block]
        return ab_ref.at[g * 4 + block, shard]

    count = [0]
    pending = []

    def copy(src, dst, device, last=True):
        s = count[0]
        count[0] += 1
        made = pltpu.make_async_remote_copy(
            src_ref=src, dst_ref=dst, send_sem=send.at[s], recv_sem=recv.at[s],
            device_id=device, device_id_type=pl.DeviceIdType.MESH,
        )
        made.start()
        if last:
            pending.append(made)
        return made

    def left(ref):
        return ref.at[:, 0:half]

    def right(ref):
        return ref.at[:, half : 2 * half]

    fetch = {}
    for o in others:
        copy(small_ref, all_small_ref.at[f], (d, o * 2 + c))
        copy(small_ref, all_small_ref.at[f], (d, o * 2 + 1 - c))
    copy(small_ref, all_small_ref.at[f], (d, mate))
    for g in range(3):
        for k, o in enumerate(others):
            fetch[g, k] = copy(own_ref.at[g * 4 + d], slot(g, d, f), (d, o * 2 + c), False)
    copy(own_ref.at[0:8], ab_ref.at[:, f], (d, mate))
    copy(own_ref.at[8:12], c_ref.at[f], (d, mate))
    keep = [
        pltpu.make_async_copy(own_ref.at[0:8], ab_ref.at[:, f], local.at[0]),
        pltpu.make_async_copy(own_ref.at[8:12], c_ref.at[f], local.at[1]),
        pltpu.make_async_copy(small_ref, all_small_ref.at[f], local.at[2]),
    ]
    for made in keep:
        made.start()
    arrived = list(fetch.values())

    units = [(g, k) for g in range(3) for k in range(nz - 1)]
    by_x, by_y, corner = {}, {}, {}
    for step in range(len(units) + 2):
        if step < len(units):
            g, k = units[step]
            shard = lax.rem(z + nz - 1 - k, nz) * 2 + c
            fetch[g, k].wait_recv()
            mine = slot(g, d, shard)
            by_x[step] = copy(mine, mine, (flip_x, f), False)
            by_y[step] = copy(mine, mine, (flip_y, f), False)
            copy(mine, mine, (d, mate))
        if 1 <= step <= len(units):
            g, k = units[step - 1]
            shard = lax.rem(z + nz - 1 - k, nz) * 2 + c
            by_x[step - 1].wait_recv()
            theirs = slot(g, flip_x, shard)
            first = copy(right(theirs), right(theirs), (flip_y, f), False)
            copy(theirs, theirs, (d, mate))
            by_y[step - 1].wait_recv()
            theirs = slot(g, flip_y, shard)
            second = copy(left(theirs), left(theirs), (flip_x, f), False)
            copy(theirs, theirs, (d, mate))
            corner[step - 1] = (first, second)
        if step >= 2:
            g, k = units[step - 2]
            shard = lax.rem(z + nz - 1 - k, nz) * 2 + c
            for made in corner[step - 2]:
                made.wait_recv()
            theirs = slot(g, flip_xy, shard)
            copy(theirs, theirs, (d, mate))
    arrived += list(by_x.values()) + list(by_y.values())
    arrived += [made for both in corner.values() for made in both]
    for made in arrived:
        made.wait_send()
    for made in pending:
        made.wait()
    for made in keep:
        made.wait()


def gather_copies(nz):
    return (2 * (nz - 1) + 1) + 3 * (nz - 1) + 2 + 3 * (nz - 1) * 8


def gather_weights(own, small, nz):
    r, width = own.shape[1:]
    copies = gather_copies(nz)
    any_spec = pl.BlockSpec(memory_space=pl.ANY)
    vmem = pl.BlockSpec(memory_space=pltpu.VMEM)
    return pl.pallas_call(
        partial(gather_kernel, nz, small.shape[0]),
        in_specs=[vmem, vmem],
        out_specs=[any_spec, any_spec, any_spec],
        out_shape=[
            jax.ShapeDtypeStruct((8, 2 * nz, r, width), BF16),
            jax.ShapeDtypeStruct((2 * nz, 4, r, width), BF16),
            jax.ShapeDtypeStruct((2 * nz,) + small.shape, BF16),
        ],
        scratch_shapes=[
            pltpu.SemaphoreType.DMA((copies,)),
            pltpu.SemaphoreType.DMA((copies,)),
            pltpu.SemaphoreType.DMA((3,)),
        ],
        compiler_params=pltpu.CompilerParams(
            collective_id=0, has_side_effects=True, vmem_limit_bytes=16 * 1024 * 1024
        ),
        name="gather_weights",
    )(own, small)


def core_split(res_ref, core, r, nz, send_ref, keep_ref):
    for i in range(nz):
        base = i * 2 * r
        send_ref[0, i] = res_ref[pl.ds(pl.multiple_of(base + (1 - core) * r, 8), r), :].astype(BF16)
        keep_ref[0, i] = res_ref[pl.ds(pl.multiple_of(base + core * r, 8), r), :].astype(BF16)


def grad_up_kernel(nz, r, ids_ref, a_ref, b_ref, send_ref, keep_ref, res_ref):
    res_ref[...] = mm_tn(a_ref[...], b_ref[...])
    core_split(res_ref, ids_ref[2], r, nz, send_ref, keep_ref)


def grad_up_split(ids, a, b, nz):
    rows, m = a.shape
    blocks = b.shape[1] // m
    r = m // (2 * nz)
    half = jax.ShapeDtypeStruct((blocks, nz, r, m), BF16)
    out = pl.BlockSpec((1, nz, r, m), lambda i, ids: (i, 0, 0, 0))
    return pl.pallas_call(
        partial(grad_up_kernel, nz, r),
        grid_spec=pltpu.PrefetchScalarGridSpec(
            num_scalar_prefetch=1,
            grid=(blocks,),
            in_specs=[
                pl.BlockSpec((rows, m), lambda i, ids: (0, 0), pipeline_mode=pl.Buffered(1)),
                pl.BlockSpec((rows, m), lambda i, ids: (0, i)),
            ],
            out_specs=[out, out],
            scratch_shapes=[pltpu.VMEM((m, m), F32)],
        ),
        out_shape=[half, half],
        compiler_params=params(),
        cost_estimate=cost(2 * rows * m * b.shape[1], 2 * (rows * m + rows * b.shape[1] + m * b.shape[1])),
        name="grad_up",
    )(ids, a, b)


def grad_attn_kernel(nz, r, ids_ref, a_ref, o_ref, q_ref, k_ref, v_ref, y_ref, send_ref, keep_ref, res_ref):
    step = pl.program_id(0)
    for i, (left, right) in enumerate(((a_ref, q_ref), (a_ref, k_ref), (a_ref, v_ref), (o_ref, y_ref))):
        @pl.when(step == i)
        def _():
            res_ref[...] = mm_tn(left[...], right[...])
    core_split(res_ref, ids_ref[2], r, nz, send_ref, keep_ref)


def grad_attn_split(ids, a1, o, dq, dk, dv, dy, nz):
    rows, m = a1.shape
    r = m // (2 * nz)
    half = jax.ShapeDtypeStruct((4, nz, r, m), BF16)
    out = pl.BlockSpec((1, nz, r, m), lambda i, ids: (i, 0, 0, 0))
    full = pl.BlockSpec((rows, m), lambda i, ids: (0, 0), pipeline_mode=pl.Buffered(1))
    return pl.pallas_call(
        partial(grad_attn_kernel, nz, r),
        grid_spec=pltpu.PrefetchScalarGridSpec(
            num_scalar_prefetch=1,
            grid=(4,),
            in_specs=[full] * 6,
            out_specs=[out, out],
            scratch_shapes=[pltpu.VMEM((m, m), F32)],
        ),
        out_shape=[half, half],
        compiler_params=params(),
        cost_estimate=cost(8 * rows * m * m, 2 * (6 * rows * m + 4 * m * m)),
        name="grad_attn",
    )(ids, a1, o, dq, dk, dv, dy)


def grad_down_kernel(r, ids_ref, a_ref, b_ref, send_ref, keep_ref, res_ref):
    res_ref[...] = mm_tn(a_ref[...], b_ref[...])
    core = ids_ref[2]
    for j in range(send_ref.shape[1]):
        for i in range(4):
            base = j * 8 * r + i * r
            there = pl.multiple_of(base + (1 - core) * 4 * r, 8)
            here = pl.multiple_of(base + core * 4 * r, 8)
            send_ref[i, j] = res_ref[pl.ds(there, r), :].astype(BF16)
            keep_ref[i, j] = res_ref[pl.ds(here, r), :].astype(BF16)


def grad_down_split(ids, a, b, nz):
    rows, hidden = a.shape
    n = b.shape[1]
    r = hidden // (8 * nz)
    per = hidden // 4
    half = jax.ShapeDtypeStruct((4, nz, r, n), BF16)
    out = pl.BlockSpec((4, nz // 4, r, n), lambda i, ids: (0, i, 0, 0))
    return pl.pallas_call(
        partial(grad_down_kernel, r),
        grid_spec=pltpu.PrefetchScalarGridSpec(
            num_scalar_prefetch=1,
            grid=(4,),
            in_specs=[
                pl.BlockSpec((rows, per), lambda i, ids: (0, i)),
                pl.BlockSpec((rows, n), lambda i, ids: (0, 0), pipeline_mode=pl.Buffered(1)),
            ],
            out_specs=[out, out],
            scratch_shapes=[pltpu.VMEM((per, n), F32)],
        ),
        out_shape=[half, half],
        compiler_params=params(),
        cost_estimate=cost(2 * rows * hidden * n, 2 * (rows * hidden + rows * n + hidden * n)),
        name="grad_down",
    )(ids, a, b)


class Exchange:
    def __init__(self, sends, keeps, mine, core_in, x_in, y_in, x2_in, y2_in, z_in, owned, dp_in, sems):
        self.sends, self.keeps = sends, keeps
        self.mine, self.core_in = mine, core_in
        self.x_in, self.y_in, self.x2_in, self.y2_in = x_in, y_in, x2_in, y2_in
        self.z_in, self.owned, self.dp_in = z_in, owned, dp_in
        self.send_sem, self.recv_sem, self.load_sem = sems
        self.groups = len(sends)
        self.nz = mine.shape[0] // self.groups
        self.half = mine.shape[3] // 2
        self.units = self.groups * self.nz
        d = lax.axis_index("dp")
        f = lax.axis_index("fsdp")
        self.d, self.f, self.z, self.c = d, f, f // 2, f % 2
        self.x = d + 1 - 2 * (d % 2)
        self.y = lax.rem(d + 2, 4)
        self.xy = lax.rem(self.x + 2, 4)
        self.mate = self.z * 2 + 1 - self.c

    def barrier(self):
        barrier = pltpu.get_barrier_semaphore()
        partners = [(self.d, self.mate)] + [(p, self.f) for p in (self.x, self.y, self.xy)]
        partners += [(self.d, lax.rem(self.z + k, self.nz) * 2 + self.c) for k in range(1, self.nz)]
        for p in partners:
            pl.semaphore_signal(barrier, inc=1, device_id=p, device_id_type=pl.DeviceIdType.MESH)
        pl.semaphore_wait(barrier, len(partners))

    def remote(self, src, dst, index, device):
        return pltpu.make_async_remote_copy(
            src_ref=src, dst_ref=dst, send_sem=self.send_sem.at[index], recv_sem=self.recv_sem.at[index],
            device_id=device, device_id_type=pl.DeviceIdType.MESH,
        )

    def owner(self, u):
        return lax.rem(self.z + 1 + u % self.nz, self.nz)

    def core_copy(self, u):
        src = self.sends[u // self.nz].at[:, self.owner(u)]
        return self.remote(src, self.core_in.at[u], u * 8, (self.d, self.mate))

    def load(self, u):
        src = self.keeps[u // self.nz].at[:, self.owner(u)]
        return pltpu.make_async_copy(src, self.mine.at[u], self.load_sem.at[u])

    def plane_copies(self, u):
        lo, hi = slice(0, self.half), slice(self.half, 2 * self.half)
        m = self.mine.at[u]
        to_x, to_y = (self.x, self.f), (self.y, self.f)
        return [
            self.remote(m.at[self.x, :, lo], self.x_in.at[u, 0], u * 8 + 1, to_x),
            self.remote(m.at[self.y, :, hi], self.y_in.at[u, 0], u * 8 + 2, to_y),
            self.remote(m.at[self.xy, :, lo], self.x_in.at[u, 1], u * 8 + 3, to_x),
            self.remote(m.at[self.xy, :, hi], self.y_in.at[u, 1], u * 8 + 4, to_y),
        ]

    def second_copies(self, u):
        lo, hi = slice(0, self.half), slice(self.half, 2 * self.half)
        m = self.mine.at[u]
        return [
            self.remote(m.at[self.y, :, lo], self.y2_in.at[u], u * 8 + 5, (self.y, self.f)),
            self.remote(m.at[self.x, :, hi], self.x2_in.at[u], u * 8 + 6, (self.x, self.f)),
        ]

    def owner_copy(self, u):
        g, j = u // self.nz, u % self.nz
        return self.remote(
            self.mine.at[u, self.d], self.z_in.at[g, j], u * 8 + 7, (self.d, self.owner(u) * 2 + self.c)
        )

    def dp_copies(self, g):
        base = self.units * 8 + 3 * g
        return [
            self.remote(self.owned.at[g], self.dp_in.at[g, i], base + i, (p, self.f))
            for i, p in enumerate((self.x, self.y, self.xy))
        ]

    def start(self):
        for u in range(self.units):
            self.core_copy(u).start()
        for u in range(self.units):
            self.load(u).start()

    def add(self, u, block, cols, term):
        value = self.mine[u, block, :, cols].astype(F32) + term.astype(F32)
        self.mine[u, block, :, cols] = value.astype(BF16)

    def stage_one(self, u):
        self.load(u).wait()
        self.core_copy(u).wait_recv()
        for block in range(4):
            self.add(u, block, slice(None), self.core_in[u, block])
        for made in self.plane_copies(u):
            made.start()

    def stage_two(self, u):
        lo, hi = slice(0, self.half), slice(self.half, 2 * self.half)
        copies = self.plane_copies(u)
        copies[0].wait_recv()
        self.add(u, self.d, lo, self.x_in[u, 0])
        copies[1].wait_recv()
        self.add(u, self.d, hi, self.y_in[u, 0])
        copies[2].wait_recv()
        self.add(u, self.y, lo, self.x_in[u, 1])
        copies[3].wait_recv()
        self.add(u, self.x, hi, self.y_in[u, 1])
        for made in self.second_copies(u):
            made.start()

    def stage_three(self, u):
        lo, hi = slice(0, self.half), slice(self.half, 2 * self.half)
        copies = self.second_copies(u)
        copies[0].wait_recv()
        self.add(u, self.d, lo, self.y2_in[u])
        copies[1].wait_recv()
        self.add(u, self.d, hi, self.x2_in[u])
        if u % self.nz != self.nz - 1:
            self.owner_copy(u).start()

    def stage_four(self, g):
        last = g * self.nz + self.nz - 1
        total = self.mine[last, self.d].astype(F32)
        for j in range(self.nz - 1):
            self.owner_copy(g * self.nz + j).wait_recv()
            total = total + self.z_in[g, j].astype(F32)
        self.owned[g] = total.astype(BF16)
        for made in self.dp_copies(g):
            made.start()

    def blocks(self, g):
        yield self.d, self.owned[g].astype(F32)
        for i, (made, p) in enumerate(zip(self.dp_copies(g), (self.x, self.y, self.xy))):
            made.wait_recv()
            yield p, self.dp_in[g, i].astype(F32)

    def finish(self):
        for u in range(self.units):
            self.core_copy(u).wait_send()
            for made in self.plane_copies(u) + self.second_copies(u):
                made.wait_send()
            if u % self.nz != self.nz - 1:
                self.owner_copy(u).wait_send()
        for g in range(self.groups):
            for made in self.dp_copies(g):
                made.wait_send()

    def steps(self):
        return self.units + 2

    def step(self, t):
        if t < self.units:
            self.stage_one(t)
        if 1 <= t <= self.units:
            self.stage_two(t - 1)
        if 2 <= t:
            self.stage_three(t - 2)


def exchange_scratch(groups, nz, r, width, extra=0):
    units = groups * nz
    half = width // 2
    copies = units * 8 + 3 * groups + extra
    return [
        pltpu.VMEM((units, 4, r, width), BF16),
        pltpu.VMEM((units, 4, r, width), BF16),
        pltpu.VMEM((units, 2, r, half), BF16),
        pltpu.VMEM((units, 2, r, half), BF16),
        pltpu.VMEM((units, r, half), BF16),
        pltpu.VMEM((units, r, half), BF16),
        pltpu.VMEM((groups, nz - 1, r, width), BF16),
        pltpu.VMEM((groups, r, width), BF16),
        pltpu.VMEM((groups, 3, r, width), BF16),
        pltpu.SemaphoreType.DMA((copies,)),
        pltpu.SemaphoreType.DMA((copies,)),
        pltpu.SemaphoreType.DMA((units,)),
    ]


def attn_bwd_exchange_kernel(
    qa_ref, k_ref, v_ref, o_ref, do_ref, kbias_ref, up_send, up_keep, down_send, down_keep,
    dq_ref, dk_ref, dv_ref, up_ref, down_ref, mask_ref, doa_ref, dqt_ref, *scratch,
):
    ex = Exchange((down_send, up_send), (down_keep, up_keep), *scratch[:9], scratch[9:])
    pid = pl.program_id(0)
    grid = 6
    slots = 2 * grid - 1

    @pl.when(pid == 0)
    def _():
        ex.barrier()
        ex.start()

    plan = {}
    total = ex.steps()
    for t in range(total):
        plan.setdefault(1 + t * min(slots, total) // total, []).append(t)

    def between(half):
        for slot, todo in plan.items():
            if slot % 2 == half:
                @pl.when(pid == slot // 2)
                def _():
                    for t in todo:
                        ex.step(t)

    attn_bwd_kernel(
        qa_ref, k_ref, v_ref, o_ref, do_ref, kbias_ref, dq_ref, dk_ref, dv_ref, mask_ref, doa_ref, dqt_ref,
        between=between,
    )

    @pl.when(pid == grid - 1)
    def _():
        r = down_send.shape[2]
        width = down_send.shape[3]
        ex.stage_four(0)
        ex.stage_four(1)
        for block, value in ex.blocks(0):
            down_ref[pl.ds(pl.multiple_of(block * r, 8), r), :] = value
        for block, value in ex.blocks(1):
            up_ref[:, pl.ds(pl.multiple_of(block * width, 128), width)] = value
        ex.finish()


def attn_backward_exchange(qa, qkv, o, do, kbias, up_halves, down_halves, nz):
    rows, width = o.shape
    pairs = width // 128
    r = up_halves[0].shape[2]

    def part(p):
        return pl.BlockSpec((rows, 128), lambda i: (0, p * pairs + i))

    any_spec = pl.BlockSpec(memory_space=pl.ANY)
    out = pl.BlockSpec((rows, 128), lambda i: (0, i))
    shape = jax.ShapeDtypeStruct((rows, width), BF16)
    return pl.pallas_call(
        attn_bwd_exchange_kernel,
        grid=(pairs,),
        in_specs=[
            pl.BlockSpec((rows, 256), lambda i: (0, i)), part(1), part(2), part(0), part(0),
            whole(kbias.shape), any_spec, any_spec, any_spec, any_spec,
        ],
        out_specs=[out, out, out, whole((r, 4 * width)), whole((4 * r, width))],
        out_shape=[
            shape, shape, shape,
            jax.ShapeDtypeStruct((r, 4 * width), F32), jax.ShapeDtypeStruct((4 * r, width), F32),
        ],
        scratch_shapes=[
            pltpu.VMEM((rows // TILE, TILE, TILE), F32),
            pltpu.VMEM((rows, 128), BF16),
            pltpu.VMEM((128, rows), F32),
        ] + exchange_scratch(2, nz, r, width),
        compiler_params=params(collective_id=1, has_side_effects=True),
        cost_estimate=cost(20 * rows * rows * width, 18 * rows * width),
        name="attn_backward_exchange",
    )(qa, qkv, qkv, o, do, kbias, *up_halves, *down_halves)


def input_exchange_kernel(
    x_ref, dq_ref, dk_ref, dv_ref, dr_ref, w_ref, vec_ref, s_bo_ref, s_g2_ref, s_h2_ref, s_bd_ref, s_bu_ref,
    send_ref, keep_ref, out_ref, qkv_ref, wo_ref, sums_ref, small_in, *scratch,
):
    ex = Exchange((send_ref,), (keep_ref,), *scratch[:9], scratch[9:])
    pid = pl.program_id(0)
    steps = 4
    width = x_ref.shape[1]

    @pl.when(pid == 0)
    def _():
        ex.barrier()
        ex.start()
        sums_ref[...] = jnp.zeros_like(sums_ref)
        for i, ref in enumerate((s_bo_ref, s_g2_ref, s_h2_ref, s_bd_ref)):
            sums_ref[4 + i : 5 + i, :] = ref[...]
        for i in range(4):
            sums_ref[8 + i : 9 + i, :] = s_bu_ref[:, i * width : (i + 1) * width]

    xhat, inv_std = norm_forward(x_ref[...].astype(F32))
    da = mm_nt(dq_ref[...], w_ref[0])
    da += mm_nt(dk_ref[...], w_ref[1])
    da += mm_nt(dv_ref[...], w_ref[2])
    totals = (da * xhat, da, dq_ref[...].astype(F32), dv_ref[...].astype(F32))
    for i, value in enumerate(totals):
        sums_ref[i : i + 1, :] += jnp.sum(value, axis=0, keepdims=True)
    out_ref[...] = dr_ref[...] + norm_backward(da, xhat, inv_std, vec_ref[0:1, :])

    total = ex.steps()
    for slot in range(steps):
        todo = [t for t in range(total) if min(t * steps // ex.units, steps - 1) == slot]

        @pl.when(pid == slot)
        def _():
            for t in todo:
                ex.step(t)

    @pl.when(pid == steps - 1)
    def _():
        base = ex.units * 8 + 3
        hops = [(ex.d, ex.mate), (ex.x, ex.f), (ex.y, ex.f)]
        small = []

        def begin(i, device):
            made = ex.remote(sums_ref, small_in.at[i], base + i, device)
            made.start()
            small.append(made)

        begin(0, hops[0])
        ex.stage_four(0)
        for i in range(3):
            small[i].wait()
            sums_ref[...] += small_in[i]
            if i < 2:
                begin(i + 1, hops[i + 1])
        for k in range(1, ex.nz):
            begin(2 + k, (ex.d, lax.rem(ex.z + k, ex.nz) * 2 + ex.c))
        for block, value in ex.blocks(0):
            @pl.when(block < 3)
            def _():
                qkv_ref[:, pl.ds(pl.multiple_of(block * width, 128), width)] = value

            @pl.when(block == 3)
            def _():
                wo_ref[...] = value
        for made in small[3:]:
            made.wait()
        total_small = sums_ref[...]
        for k in range(1, ex.nz):
            total_small = total_small + small_in[2 + k]
        sums_ref[...] = total_small
        ex.finish()


def input_grad_exchange(x, dq, dk, dv, dr, ab, vecs, smalls, halves, nz):
    rows, width = x.shape
    tile = rows // 4
    r = halves[0].shape[2]
    row = rows_spec(tile, width)
    any_spec = pl.BlockSpec(memory_space=pl.ANY)
    return pl.pallas_call(
        input_exchange_kernel,
        grid=(4,),
        in_specs=[row, row, row, row, row, whole((3, width, width)), whole(vecs.shape)]
        + [whole(s.shape) for s in smalls] + [any_spec, any_spec],
        out_specs=[row, whole((r, 3 * width)), whole((r, width)), whole((16, width))],
        out_shape=[
            jax.ShapeDtypeStruct((rows, width), F32), jax.ShapeDtypeStruct((r, 3 * width), F32),
            jax.ShapeDtypeStruct((r, width), F32), jax.ShapeDtypeStruct((16, width), F32),
        ],
        scratch_shapes=[pltpu.VMEM((2 + nz, 16, width), F32)] + exchange_scratch(1, nz, r, width, 2 + nz),
        compiler_params=params(collective_id=2, has_side_effects=True),
        cost_estimate=cost(6 * rows * width * width, 16 * rows * width),
        name="input_grad_exchange",
    )(x, dq, dk, dv, dr, ab, vecs, *smalls, *halves)


def per_device(
    tokens, lengths, cells, cotangent, ln1_gain, ln1_bias, w_qkv, b_query, b_value, w_out, b_out,
    ln2_gain, ln2_bias, w_up, b_up, w_down, b_down,
):
    seqs, context, width = tokens.shape
    r = w_qkv.shape[0]
    nf = width // r
    nz = nf // 2
    f = lax.axis_index("fsdp")
    ids = jnp.stack([lax.axis_index("dp"), f // 2, f % 2]).astype(jnp.int32)
    vectors = (ln1_gain, ln1_bias, b_query, b_value, b_out, ln2_gain, ln2_bias, b_down, b_up)
    flat = jnp.concatenate(vectors)
    small_rows = -(-flat.shape[0] // 2048) * 16
    small = jnp.pad(flat, (0, small_rows * 128 - flat.shape[0])).reshape(small_rows, 128)
    own = jnp.stack(
        [w_qkv[:, i * width : (i + 1) * width] for i in range(3)]
        + [w_out]
        + [w_up[:, i * width : (i + 1) * width] for i in range(4)]
        + [w_down[i * r : (i + 1) * r] for i in range(4)]
    )
    ab, down_full, smalls = gather_weights(own, small, nz)
    ab = ab.reshape(8, width, width)
    down_full = down_full.reshape(4 * width, width)
    smalls = smalls.reshape(nf, -1).astype(F32)
    vecs = smalls[:, : 8 * r].reshape(nf, 8, r).transpose(1, 0, 2).reshape(8, width)
    bu = smalls[:, 8 * r : 12 * r].reshape(1, 4 * width)
    x = tokens[0]
    kbias, rbias, valid = mask_terms(lengths, cells, context)
    a1, qkv = qkv_forward(x, ab, vecs, 0.125)
    o, qa = attn_forward(qkv, kbias, rbias)
    out, dm, a2, g, du, dr, dy, do, s_g2, s_h2, s_bu, s_bd, s_bo = mlp_both(
        x, o, cotangent[0], valid, ab, down_full, vecs, bu
    )
    down_halves = grad_down_split(ids, g, dm, nz)
    up_halves = grad_up_split(ids, a2, du, nz)
    dq, dk, dv, grad_up, grad_down = attn_backward_exchange(
        qa, qkv, o, do, kbias, up_halves, down_halves, nz
    )
    attn_halves = grad_attn_split(ids, a1, o, dq, dk, dv, dy, nz)
    grad_x, grad_qkv, grad_out, sums = input_grad_exchange(
        x, dq, dk, dv, dr, ab, vecs, (s_bo, s_g2, s_h2, s_bd, s_bu), attn_halves, nz
    )
    mine = lax.dynamic_slice(sums, (0, f * r), (8, r))
    g_g1, g_h1, g_bq, g_bv, g_bo, g_g2, g_h2, g_bd = (mine[i] for i in range(8))
    g_bu = lax.dynamic_slice(sums[8:12].reshape(-1), (f * 4 * r,), (4 * r,))
    return (
        out[None], grad_x[None], g_g1, g_h1, grad_qkv, g_bq, g_bv, grad_out, g_bo, g_g2, g_h2,
        grad_up, g_bu, grad_down, g_bd,
    )


def solution(mesh):
    split = P(("dp", "fsdp"), None, None)
    vec, mat = P("fsdp"), P("fsdp", None)
    in_specs = (
        split, P(("dp", "fsdp")), P(("dp", "fsdp"), None), split,
        vec, vec, mat, vec, vec, mat, vec, vec, vec, mat, vec, mat, vec,
    )
    out_specs = (split, split, vec, vec, mat, vec, vec, mat, vec, vec, vec, mat, vec, mat, vec)
    return jax.shard_map(
        per_device, mesh=mesh, in_specs=in_specs, out_specs=out_specs, check_vma=False
    )
```

profile of v0, /device:TPU:0, one launch (start us, length us, event | category | flops | bytes accessed | tf_op | source)
XLA Modules:
  0.0 320.8 jit_solution(808423950059657487)
XLA Ops:
  0.8 1.0 bitcast_dynamic-update-slice_fusion.11
  1.8 0.9 bitcast_dynamic-update-slice_fusion.10
  2.7 0.9 bitcast_dynamic-update-slice_fusion.9
  3.6 0.9 bitcast_dynamic-update-slice_fusion.8
  4.5 0.9 bitcast_dynamic-update-slice_fusion.7
  5.5 0.9 bitcast_dynamic-update-slice_fusion.6
  6.7 68.7 %gather_weights.1 = (bf16[8,8,96,768]{3,2,1,0:T(8,128)(2,1)S(1)}, bf16[8,4,96,768]{3,2,1,0:T(8,128)(2,1)S(1)}, bf16[8,16,128]{2,1,0:T(8,128)(2,1)S(1)}) custom-call(bf16[12,96,768]{2,1,0:T(8,128)(2,1)S(1)} %bitcast_dynamic-update-slice_fusion.own_ref, bf16[16,128]{1,0:T(8,128)(2,1)S(1)} %pad_bitcast_fusion.small_ref), custom_call_target="tpu_custom_call" | custom-call | tf_op jit(solution)/shard_map/gather_weights/pallas_call | solution.py:541
  75.5 3.7 %copy-done = bf16[8,8,96,768]{3,2,1,0:T(8,128)(2,1)} copy-done((bf16[8,8,96,768]{3,2,1,0:T(8,128)(2,1)}, bf16[8,8,96,768]{3,2,1,0:T(8,128)(2,1)S(1)}, u32[]{:S(2)}) %copy-start) | copy-done | bytes 9437208
  79.1 2.2 copy-done.1
  81.5 0.7 reshape.81.vec_ref
  82.2 8.4 %qkv_forward.1 = (bf16[1024,768]{1,0:T(8,128)(2,1)}, bf16[1024,2304]{1,0:T(8,128)(2,1)}) custom-call(bf16[1024,768]{1,0:T(8,128)(2,1)} %bitcast.71, bf16[8,768,768]{2,1,0:T(8,128)(2,1)} %bitcast.65, f32[8,768]{1,0:T(8,128)} %reshape.81.vec_ref), custom_call_target="tpu_custom_call" | custom-call | flops 3623878656 | bytes 9437184 | tf_op jit(solution)/shard_map/qkv_forward/pallas_call | solution.py:95
  91.3 0.9 broadcast_in_dim.33.kbias_ref
  92.2 0.6 and_select_fusion.rbias_ref
  92.8 23.7 %attn_forward.1 = (bf16[1024,768]{1,0:T(8,128)(2,1)}, bf16[1024,1536]{1,0:T(8,128)(2,1)}) custom-call(bf16[1024,2304]{1,0:T(8,128)(2,1)} %get-tuple-element.52.q_ref.k_ref.v_ref, bf16[1024,2304]{1,0:T(8,128)(2,1)} %get-tuple-element.52.q_ref.k_ref.v_ref, bf16[1024,2304]{1,0:T(8,128)(2,1)} %get-tuple-element.52.q_ref.k_ref.v_ref, ...), custom_call_target="tpu_custom_call" | custom-call | flops 6442450944 | bytes 9437184 | tf_op jit(solution)/shard_map/attn_forward/pallas_call | solution.py:173
  116.5 1.0 broadcast_in_dim.36.valid_ref
  117.5 0.6 copy.34
  118.1 34.8 %mlp_both.1 = (bf16[1024,768]{1,0:T(8,128)(2,1)}, bf16[1024,768]{1,0:T(8,128)(2,1)}, bf16[1024,768]{1,0:T(8,128)(2,1)}, bf16[1024,3072]{1,0:T(8,128)(2,1)}, bf16...) custom-call(bf16[1024,768]{1,0:T(8,128)(2,1)} %bitcast.72, ...), custom_call_target="tpu_custom_call" | custom-call | flops 21743271936 | bytes 56623104 | tf_op jit(solution)/shard_map/mlp_both/pallas_call | solution.py:356
  153.0 0.6 pad_add_fusion.ids_ref
  153.5 10.0 %grad_up.1 = (bf16[4,4,96,768]{3,2,1,0:T(8,128)(2,1)}, bf16[4,4,96,768]{3,2,1,0:T(8,128)(2,1)}) custom-call(s32[3]{0:T(128)} %pad_add_fusion.ids_ref, bf16[1024,768]{1,0:T(8,128)(2,1)} %get-tuple-element.58.a_ref, bf16[1024,3072]{1,0:T(8,128)(2,1)} %get-tuple-element.59.b_ref), custom_call_target="tpu_custom_call" | custom-call | flops 4831838208 | bytes 12582912 | tf_op jit(solution)/shard_map/grad_up/pallas_call | solution.py:580
  163.6 10.2 %grad_down.1 = (bf16[4,4,96,768]{3,2,1,0:T(8,128)(2,1)}, bf16[4,4,96,768]{3,2,1,0:T(8,128)(2,1)}) custom-call(s32[3]{0:T(128)} %pad_add_fusion.ids_ref, bf16[1024,3072]{1,0:T(8,128)(2,1)} %get-tuple-element.62.a_ref, bf16[1024,768]{1,0:T(8,128)(2,1)} %get-tuple-element.63.b_ref), custom_call_target="tpu_custom_call" | custom-call | flops 4831838208 | bytes 12582912 | tf_op jit(solution)/shard_map/grad_down/pallas_call | solution.py:649
  173.8 72.9 %attn_backward_exchange.1 = (bf16[1024,768]{1,0:T(8,128)(2,1)}, bf16[1024,768]{1,0:T(8,128)(2,1)}, bf16[1024,768]{1,0:T(8,128)(2,1)}, f32[96,3072]{1,0:T(8,128)}, f32[384,768]{1,0:T(8,128)}) custom-call(bf16[1024,1536]{1,0:T(8,128)(2,1)} %get-tuple-element.56.qa_ref, bf16[1024,2304]{1,0:T(8,128)(2,1)} %get-tuple-element.52.q_ref.k_ref.v_ref, ...), custom_call_target="tpu_custom_call" | custom-call | flops 16106127360 | bytes 14155776 | tf_op jit(solution)/shard_map/attn_backward_exchange/pallas_call | solution.py:901
  246.6 12.1 %grad_attn.1 = (bf16[4,4,96,768]{3,2,1,0:T(8,128)(2,1)}, bf16[4,4,96,768]{3,2,1,0:T(8,128)(2,1)}) custom-call(s32[3]{0:T(128)} %pad_add_fusion.ids_ref, bf16[1024,768]{1,0:T(8,128)(2,1)} %get-tuple-element.75.a_ref, bf16[1024,768]{1,0:T(8,128)(2,1)} %get-tuple-element.53.o_ref, bf16[1024,768]{1,0:T(8,128)(2,1)} %get-tuple-element.66.q_ref.dq_ref, ...), custom_call_target="tpu_custom_call" | custom-call | flops 4831838208 | bytes 14155776 | tf_op jit(solution)/shard_map/grad_attn/pallas_call | solution.py:614
  258.7 51.6 %input_grad_exchange.1 = (f32[1024,768]{1,0:T(8,128)}, f32[96,2304]{1,0:T(8,128)}, f32[96,768]{1,0:T(8,128)}, f32[16,768]{1,0:T(8,128)}) custom-call(bf16[1024,768]{1,0:T(8,128)(2,1)} %bitcast.73, bf16[1024,768]{1,0:T(8,128)(2,1)} %get-tuple-element.66.q_ref.dq_ref, bf16[1024,768]{1,0:T(8,128)(2,1)} %get-tuple-element.67.k_ref.dk_ref, ...), custom_call_target="tpu_custom_call" | custom-call | flops 3623878656 | bytes 12582912 | tf_op jit(solution)/shard_map/input_grad_exchange/pallas_call | solution.py:1004
  310.3 0.8 constant_dynamic-slice_fusion
  311.1 0.5 slice_bitcast_fusion.1
  311.6 0.7 slice.86
  312.4 0.7 dynamic_slice.7
  313.1 3.8 %copy.54 = f32[1,1024,768]{2,1,0:T(8,128)} copy(f32[1,1024,768]{2,1,0:T(8,128)} %bitcast.70) | data formatting | bytes 6291456
  316.9 0.9 copy.55
  318.0 0.7 copy.56
  318.7 1.0 copy.57
  319.8 1.0 copy.58
  (52 shorter events, 0.6 us)
Async XLA Ops:
  0.7 5.7 %copy-start.5 = (bf16[96,3072]{1,0:T(8,128)(2,1)S(1)}, bf16[96,3072]{1,0:T(8,128)(2,1)}, u32[]{:S(2)}) copy-start(bf16[96,3072]{1,0:T(8,128)(2,1)} %param.30) | copy-start | bytes 1769476
  0.7 5.8 %copy-start.6 = (bf16[384,768]{1,0:T(8,128)(2,1)S(1)}, bf16[384,768]{1,0:T(8,128)(2,1)}, u32[]{:S(2)}) copy-start(bf16[384,768]{1,0:T(8,128)(2,1)} %param.32) | copy-start | bytes 1769476
  0.7 5.9 %copy-start.9 = (bf16[384]{0:T(512)(128)(2,1)S(1)}, bf16[384]{0:T(512)(128)(2,1)}, u32[]{:S(2)}) copy-start(bf16[384]{0:T(512)(128)(2,1)} %param.31) | copy-start | bytes 2308
  0.7 5.9 %copy-start.10 = (bf16[96]{0:T(256)(128)(2,1)S(1)}, bf16[96]{0:T(256)(128)(2,1)}, u32[]{:S(2)}) copy-start(bf16[96]{0:T(256)(128)(2,1)} %param.21) | copy-start | bytes 580
  0.7 5.9 %copy-start.11 = (bf16[96]{0:T(256)(128)(2,1)S(1)}, bf16[96]{0:T(256)(128)(2,1)}, u32[]{:S(2)}) copy-start(bf16[96]{0:T(256)(128)(2,1)} %param.22) | copy-start | bytes 580
  0.7 5.9 %copy-start.12 = (bf16[96]{0:T(256)(128)(2,1)S(1)}, bf16[96]{0:T(256)(128)(2,1)}, u32[]{:S(2)}) copy-start(bf16[96]{0:T(256)(128)(2,1)} %param.24) | copy-start | bytes 580
  0.7 5.9 %copy-start.13 = (bf16[96]{0:T(256)(128)(2,1)S(1)}, bf16[96]{0:T(256)(128)(2,1)}, u32[]{:S(2)}) copy-start(bf16[96]{0:T(256)(128)(2,1)} %param.25) | copy-start | bytes 580
  0.7 5.9 %copy-start.14 = (bf16[96]{0:T(256)(128)(2,1)S(1)}, bf16[96]{0:T(256)(128)(2,1)}, u32[]{:S(2)}) copy-start(bf16[96]{0:T(256)(128)(2,1)} %param.27) | copy-start | bytes 580
  0.7 5.9 %copy-start.15 = (bf16[96]{0:T(256)(128)(2,1)S(1)}, bf16[96]{0:T(256)(128)(2,1)}, u32[]{:S(2)}) copy-start(bf16[96]{0:T(256)(128)(2,1)} %param.28) | copy-start | bytes 580
  0.7 5.9 %copy-start.16 = (bf16[96]{0:T(256)(128)(2,1)S(1)}, bf16[96]{0:T(256)(128)(2,1)}, u32[]{:S(2)}) copy-start(bf16[96]{0:T(256)(128)(2,1)} %param.29) | copy-start | bytes 580
  0.8 5.9 %copy-start.17 = (bf16[96]{0:T(256)(128)(2,1)S(1)}, bf16[96]{0:T(256)(128)(2,1)}, u32[]{:S(2)}) copy-start(bf16[96]{0:T(256)(128)(2,1)} %param.33) | copy-start | bytes 580
  75.5 3.7 %copy-start = (bf16[8,8,96,768]{3,2,1,0:T(8,128)(2,1)}, bf16[8,8,96,768]{3,2,1,0:T(8,128)(2,1)S(1)}, u32[]{:S(2)}) copy-start(bf16[8,8,96,768]{3,2,1,0:T(8,128)(2,1)S(1)} %get-tuple-element.50) | copy-start | bytes 28311556
  79.1 2.2 copy-start.1
  82.2 8.4 %copy-start.8 = (s32[1,1024]{1,0:T(1,128)S(1)}, s32[1,1024]{1,0:T(1,128)}, u32[]{:S(2)}) copy-start(s32[1,1024]{1,0:T(1,128)} %param.19) | copy-start | bytes 12292
  313.1 3.8 %copy-start.4 = (f32[96,2304]{1,0:T(8,128)S(1)}, f32[96,2304]{1,0:T(8,128)}, u32[]{:S(2)}) copy-start(f32[96,2304]{1,0:T(8,128)} %get-tuple-element.112) | copy-start | bytes 2654212
  316.9 1.1 copy-start.7
  316.9 1.8 copy-start.3
  318.0 1.7 copy-start.2
where the time goes:
time: 321 us
  Pallas kernels  292 us (91%)
  local copies, waits for them, and re-layouts  25.5 us (8%)
    pallas_call x1, Pallas kernels, attn_backward_exchange(): pl.pallas_call(attn_bwd_exchange_kernel, grid=(pairs,), in_specs=[pl.Bloc...  72.9 us
    pallas_call x1, Pallas kernels, gather_weights(): pl.pallas_call(partial(gather_kernel, nz, small.shape[0]), in_specs=[vmem...  68.7 us
    pallas_call x1, Pallas kernels, input_grad_exchange(): pl.pallas_call(input_exchange_kernel, grid=(4,), in_specs=[row, row, row,...  51.6 us
    pallas_call x1, Pallas kernels, mlp_both(): pl.pallas_call(mlp_kernel, grid=(rows // TILE,), in_specs=[row, row, row,...  34.8 us
    pallas_call x1, Pallas kernels, attn_forward(): pl.pallas_call(attn_fwd_kernel, grid=(pairs,), in_specs=[part(0), part(1)...  23.7 us
    unnamed x55, local copies, waits for them, and re-layouts  20 us
    pallas_call x1, Pallas kernels, grad_attn_split(): pl.pallas_call(partial(grad_attn_kernel, nz, r), grid_spec=pltpu.Prefetch...  12.1 us
    pallas_call x1, Pallas kernels, grad_down_split(): pl.pallas_call(partial(grad_down_kernel, r), grid_spec=pltpu.PrefetchScal...  10.2 us

commit v1 on v0

--- a/solution.py
+++ b/solution.py
@@ -115,11 +115,11 @@
     return first, second, third
 
 
-def attn_fwd_kernel(q_ref, k_ref, v_ref, kbias_ref, rbias_ref, o_ref, qa_ref, mask_ref):
+def attn_fwd_kernel(q_ref, k_ref, v_ref, kbias_ref, rbias_ref, o_ref, qa_ref, mask_ref, between=None):
     blocks = q_ref.shape[0] // TILE
     lane = lax.broadcasted_iota(jnp.int32, (1, 128), 1)
 
-    @pl.when(pl.program_id(0) == 0)
+    @pl.when((pl.program_id(0) == 0) & (between is None))
     def _():
         row = lax.broadcasted_iota(jnp.int32, (TILE, TILE), 0)
         col = lax.broadcasted_iota(jnp.int32, (TILE, TILE), 1)
@@ -133,6 +133,8 @@
         base = 64 * head
         extra = 64 - base
         own = (lane >= base) & (lane < base + 64)
+        if between is not None:
+            between(head)
         k_off = jnp.where(own, k_ref[...], jnp.where(lane == extra, kbias_ref[...], zero))
         for i in range(blocks):
             here = slice(i * TILE, (i + 1) * TILE)
@@ -262,41 +264,8 @@
             dq_ref[...] = dq
 
 
-def attn_backward(qa, qkv, o, do, kbias, first_pair, pair_count):
-    rows, width = o.shape
-    pairs = width // 128
-
-    def part(p):
-        return pl.BlockSpec((rows, 128), lambda i: (0, p * pairs + first_pair + i))
-
-    out = pl.BlockSpec((rows, 128), lambda i: (0, i))
-    shape = jax.ShapeDtypeStruct((rows, 128 * pair_count), BF16)
-    return pl.pallas_call(
-        attn_bwd_kernel,
-        grid=(pair_count,),
-        in_specs=[
-            pl.BlockSpec((rows, 256), lambda i: (0, first_pair + i)),
-            part(1),
-            part(2),
-            part(0),
-            part(0),
-            whole(kbias.shape),
-        ],
-        out_specs=[out, out, out],
-        out_shape=[shape, shape, shape],
-        scratch_shapes=[
-            pltpu.VMEM((rows // TILE, TILE, TILE), F32),
-            pltpu.VMEM((rows, 128), BF16),
-            pltpu.VMEM((128, rows), F32),
-        ],
-        compiler_params=params(),
-        cost_estimate=cost(20 * rows * rows * 128 * pair_count, 18 * rows * 128 * pair_count),
-        name="attn_backward",
-    )(qa, qkv, qkv, o, do, kbias)
-
-
 def mlp_kernel(
-    x_ref, o_ref, cot_ref, valid_ref, wo_ref, wu_ref, wd_ref, vec_ref, bu_ref,
+    x_ref, o_ref, cot_ref, length_ref, wo_ref, wu_ref, wd_ref, vec_ref, bu_ref,
     out_ref, dm_ref, a2_ref, g_ref, du_ref, dr_ref, dy_ref, do_ref,
     s_gain_ref, s_shift_ref, s_bu_ref, s_bd_ref, s_bo_ref,
 ):
@@ -307,7 +276,8 @@
     xhat, inv_std = norm_forward(middle)
     a2 = (xhat * gain + shift).astype(BF16)
     a2_ref[...] = a2
-    dout = cot_ref[...].astype(F32) * valid_ref[:, 0:1]
+    row = lax.broadcasted_iota(jnp.int32, middle.shape, 0) + pl.program_id(0) * middle.shape[0]
+    dout = jnp.where(row < length_ref[0], cot_ref[...].astype(F32), 0.0)
     dm = dout.astype(BF16)
     dm_ref[...] = dm
     out = middle + bd
@@ -342,7 +312,7 @@
     do_ref[...] = mm_nt(dy, wo_ref[0]).astype(BF16)
 
 
-def mlp_both(x, o, cot, valid, ab, w_down, vecs, b_up):
+def mlp_both(x, o, cot, lengths, ab, w_down, vecs, b_up):
     rows, width = x.shape
     hidden = w_down.shape[0]
     row = rows_spec(TILE, width)
@@ -357,7 +327,7 @@
         mlp_kernel,
         grid=(rows // TILE,),
         in_specs=[
-            row, row, row, rows_spec(TILE, 128),
+            row, row, row, pl.BlockSpec(memory_space=pltpu.SMEM),
             pl.BlockSpec((1, width, width), lambda i: (3, 0, 0), pipeline_mode=pl.Buffered(1)),
             pl.BlockSpec((4, width, width), lambda i: (1, 0, 0), pipeline_mode=pl.Buffered(1)),
             whole(w_down.shape), whole(vecs.shape), whole(b_up.shape),
@@ -373,56 +343,13 @@
         compiler_params=params(),
         cost_estimate=cost(rows * width * (8 * hidden + 4 * width), 24 * rows * width + 12 * rows * hidden),
         name="mlp_both",
-    )(x, o, cot, valid, ab, ab, w_down, vecs, b_up)
-
-
-def input_kernel(
-    x_ref, dq_ref, dk_ref, dv_ref, dr_ref, w_ref, vec_ref, out_ref, s_gain_ref, s_shift_ref, s_bq_ref, s_bv_ref
-):
-    width = x_ref.shape[1]
-    xhat, inv_std = norm_forward(x_ref[...].astype(F32))
-    da = mm_nt(dq_ref[...], w_ref[0])
-    da += mm_nt(dk_ref[...], w_ref[1])
-    da += mm_nt(dv_ref[...], w_ref[2])
-    first = pl.program_id(0) == 0
-
-    def add_sum(ref, value):
-        part = jnp.sum(value, axis=0, keepdims=True)
-        ref[...] = jnp.where(first, part, ref[...] + part)
-
-    add_sum(s_gain_ref, da * xhat)
-    add_sum(s_shift_ref, da)
-    add_sum(s_bq_ref, dq_ref[...].astype(F32))
-    add_sum(s_bv_ref, dv_ref[...].astype(F32))
-    out_ref[...] = dr_ref[...] + norm_backward(da, xhat, inv_std, vec_ref[0:1, :])
-
-
-def input_grad(x, dq, dk, dv, dr, ab, vecs):
-    rows, width = x.shape
-    row = rows_spec(TILE, width)
-    acc = pl.BlockSpec((1, width), lambda i: (0, 0))
-    vec = jax.ShapeDtypeStruct((1, width), F32)
-    return pl.pallas_call(
-        input_kernel,
-        grid=(rows // TILE,),
-        in_specs=[row, row, row, row, row, whole((3, width, width)), whole(vecs.shape)],
-        out_specs=[row, acc, acc, acc, acc],
-        out_shape=[jax.ShapeDtypeStruct((rows, width), F32), vec, vec, vec, vec],
-        compiler_params=params(),
-        cost_estimate=cost(6 * rows * width * width, 16 * rows * width),
-        name="input_grad",
-    )(x, dq, dk, dv, dr, ab, vecs)
+    )(x, o, cot, lengths, ab, ab, w_down, vecs, b_up)
 
 
 def mask_terms(lengths, cells, context):
     usable = (jnp.arange(context) < lengths[0]) & (cells[0] == 1)
     bias = jnp.where(usable, 0.0, MASKED)
-    kbias = jnp.broadcast_to(bias.astype(BF16)[:, None], (context, 128))
-    rbias = bias[None, :]
-    valid = jnp.broadcast_to(
-        (jnp.arange(context) < lengths[0]).astype(F32)[:, None], (context, 128)
-    )
-    return kbias, rbias, valid
+    return jnp.broadcast_to(bias.astype(BF16)[:, None], (context, 128)), bias[None, :]
 
 
 def gather_kernel(nz, n_small, own_ref, small_ref, ab_ref, c_ref, all_small_ref, send, recv, local):
@@ -559,6 +486,310 @@
     )(own, small)
 
 
+def head_kernel(
+    nz, slots_of, wqkv_ref, wout_ref, wup_ref, wdown_ref, small_ref, x_ref, cells_ref, length_ref,
+    ab_ref, c_ref, vecs_ref, bu_ref, kbias_ref, a1_ref, qkv_ref, o_ref, qa_ref,
+    own, attn_w, up_w, down_w, rbias_ref, all_small, mask_ref, send, recv, local,
+):
+    pid = pl.program_id(0)
+    d = lax.axis_index("dp")
+    f = lax.axis_index("fsdp")
+    z, c = f // 2, f % 2
+    r, width = own.shape[1:]
+    half = width // 2
+    rows = x_ref.shape[0]
+    mate = z * 2 + (1 - c)
+    flip_x = d + 1 - 2 * (d % 2)
+    flip_y = lax.rem(d + 2, 4)
+    flip_xy = lax.rem(flip_x + 2, 4)
+    others = [lax.rem(z + k, nz) for k in range(1, nz)]
+
+    def slot(g, block, shard):
+        if g == 0:
+            return attn_w.at[block, shard]
+        if g == 1:
+            return up_w.at[block, shard]
+        return down_w.at[shard, block]
+
+    def remote(src, dst, index, device):
+        return pltpu.make_async_remote_copy(
+            src_ref=src, dst_ref=dst, send_sem=send.at[index], recv_sem=recv.at[index],
+            device_id=device, device_id_type=pl.DeviceIdType.MESH,
+        )
+
+    units = [(g, k) for g in range(3) for k in range(nz - 1)]
+    own_base = len(units) * 9
+    small_base = own_base + 3
+
+    def shard_of(k):
+        return lax.rem(z + nz - 1 - k, nz) * 2 + c
+
+    def fetch(u):
+        g, k = units[u]
+        return remote(own.at[g * 4 + d], slot(g, d, f), u * 9, (d, others[k] * 2 + c))
+
+    def stage_one(u):
+        g, k = units[u]
+        mine = slot(g, d, shard_of(k))
+        return [
+            remote(mine, mine, u * 9 + 1, (flip_x, f)),
+            remote(mine, mine, u * 9 + 2, (flip_y, f)),
+            remote(mine, mine, u * 9 + 3, (d, mate)),
+        ]
+
+    def stage_two(u):
+        g, k = units[u]
+        from_x, from_y = slot(g, flip_x, shard_of(k)), slot(g, flip_y, shard_of(k))
+        right, left = from_x.at[:, half : 2 * half], from_y.at[:, 0:half]
+        return [
+            remote(right, right, u * 9 + 4, (flip_y, f)),
+            remote(from_x, from_x, u * 9 + 5, (d, mate)),
+            remote(left, left, u * 9 + 6, (flip_x, f)),
+            remote(from_y, from_y, u * 9 + 7, (d, mate)),
+        ]
+
+    def stage_three(u):
+        g, k = units[u]
+        corner = slot(g, flip_xy, shard_of(k))
+        return remote(corner, corner, u * 9 + 8, (d, mate))
+
+    def own_copies():
+        return [
+            remote(own.at[0:4], attn_w.at[:, f], own_base, (d, mate)),
+            remote(own.at[4:8], up_w.at[:, f], own_base + 1, (d, mate)),
+            remote(own.at[8:12], down_w.at[f], own_base + 2, (d, mate)),
+        ]
+
+    def own_keeps():
+        return [
+            pltpu.make_async_copy(own.at[0:4], attn_w.at[:, f], local.at[0]),
+            pltpu.make_async_copy(own.at[4:8], up_w.at[:, f], local.at[1]),
+            pltpu.make_async_copy(own.at[8:12], down_w.at[f], local.at[2]),
+        ]
+
+    def small_copies():
+        there = [(d, o * 2 + e) for o in others for e in (c, 1 - c)] + [(d, mate)]
+        return [remote(small_ref, all_small.at[f], small_base + i, p) for i, p in enumerate(there)]
+
+    def outward(g):
+        if g == 0:
+            return pltpu.make_async_copy(attn_w, ab_ref.at[0:4], local.at[3])
+        if g == 1:
+            return pltpu.make_async_copy(up_w, ab_ref.at[4:8], local.at[4])
+        return pltpu.make_async_copy(down_w, c_ref, local.at[17])
+
+    def event(t, lo, hi):
+        if lo <= t < hi:
+            fetch(t).wait_recv()
+            if t < nz - 1:
+                fetch(nz - 1 + t).start()
+            for made in stage_one(t):
+                made.start()
+        if lo <= t - 1 < hi:
+            one, two = stage_one(t - 1), stage_two(t - 1)
+            one[0].wait_recv()
+            two[0].start()
+            two[1].start()
+            one[1].wait_recv()
+            two[2].start()
+            two[3].start()
+        if lo <= t - 2 < hi:
+            two = stage_two(t - 2)
+            two[0].wait_recv()
+            two[2].wait_recv()
+            stage_three(t - 2).start()
+
+    def mates_done(lo, hi):
+        for u in range(lo, hi):
+            stage_one(u)[2].wait_recv()
+            stage_two(u)[1].wait_recv()
+            stage_two(u)[3].wait_recv()
+            stage_three(u).wait_recv()
+
+    @pl.when(pid == 0)
+    def _():
+        fill = []
+        for i in range(12):
+            if i < 3:
+                src = wqkv_ref.at[:, i * width : (i + 1) * width]
+            elif i == 3:
+                src = wout_ref
+            elif i < 8:
+                src = wup_ref.at[:, (i - 4) * width : (i - 3) * width]
+            else:
+                src = wdown_ref.at[(i - 8) * r : (i - 7) * r, :]
+            fill.append(pltpu.make_async_copy(src, own.at[i], local.at[5 + i]))
+        for made in fill:
+            made.start()
+        barrier = pltpu.get_barrier_semaphore()
+        partners = [(flip_x, f), (flip_y, f), (d, mate)]
+        for o in others:
+            partners += [(d, o * 2 + c), (d, o * 2 + 1 - c)]
+        for p in partners:
+            pl.semaphore_signal(barrier, inc=1, device_id=p, device_id_type=pl.DeviceIdType.MESH)
+        for made in fill:
+            made.wait()
+        pl.semaphore_wait(barrier, len(partners))
+        for made in small_copies():
+            made.start()
+        for u in range(nz - 1):
+            fetch(u).start()
+        for made in own_copies() + own_keeps():
+            made.start()
+        all_small[f] = small_ref[...]
+
+        usable = (lax.broadcasted_iota(jnp.int32, (1, rows), 1) < length_ref[0]) & (cells_ref[...] == 1)
+        rbias_ref[...] = jnp.where(usable, 0.0, MASKED)
+        kbias_ref[...] = jnp.broadcast_to(rbias_ref[...], (128, rows)).T.astype(BF16)
+        row = lax.broadcasted_iota(jnp.int32, (TILE, TILE), 0)
+        col = lax.broadcasted_iota(jnp.int32, (TILE, TILE), 1)
+        for i in range(rows // TILE):
+            keys = rbias_ref[:, i * TILE : (i + 1) * TILE]
+            mask_ref[i] = jnp.where(row == col, 0.0, jnp.where(row > col, keys, MASKED))
+
+        for made in small_copies():
+            made.wait_recv()
+        lane = lax.broadcasted_iota(jnp.int32, (128, width), 0)
+        at = lax.broadcasted_iota(jnp.int32, (128, width), 1)
+        vecs = jnp.zeros((16, width), F32)
+        for shard in range(2 * nz):
+            spot = ((at == lane + shard * r) & (lane < r)).astype(BF16)
+            vecs += mm(all_small[shard], spot)
+        vecs_ref[...] = vecs
+        lane = lax.broadcasted_iota(jnp.int32, (128, 4 * r), 0)
+        at = lax.broadcasted_iota(jnp.int32, (128, 4 * r), 1)
+        for shard in range(2 * nz):
+            part = jnp.zeros((16, 4 * r), F32)
+            for j in range(4):
+                spot = ((at == lane + j * r) & (lane < r)).astype(BF16)
+                part = part + mm(pltpu.roll(all_small[shard].astype(F32), 8 - j, 0).astype(BF16), spot)
+            bu_ref[:, shard * 4 * r : (shard + 1) * 4 * r] = part[0:1]
+        gain, shift = vecs_ref[0:1, :], vecs_ref[1:2, :]
+        for i in range(rows // TILE):
+            here = slice(i * TILE, (i + 1) * TILE)
+            xhat, _ = norm_forward(x_ref[here, :].astype(F32))
+            a1_ref[here, :] = (xhat * gain + shift).astype(BF16)
+
+        for t in range(nz + 1):
+            event(t, 0, nz - 1)
+        own_copies()[0].wait_recv()
+        own_keeps()[0].wait()
+        mates_done(0, nz - 1)
+        outward(0).start()
+        for u in range(2 * nz - 2, len(units)):
+            fetch(u).start()
+
+    def between(index):
+        if index == 15:
+            mates_done(nz - 1, 2 * nz - 2)
+            own_copies()[1].wait_recv()
+            own_keeps()[1].wait()
+            outward(1).start()
+        for t in slots_of.get(index, ()):
+            event(nz - 1 + t, nz - 1, len(units))
+
+    for i in range(4):
+        @pl.when(pid == 1 + i)
+        def _():
+            between(i)
+
+    @pl.when((pid >= 1) & (pid < 5))
+    def _():
+        size = rows // 4
+        here = pl.ds(pl.multiple_of((pid - 1) * size, size), size)
+        a1 = a1_ref[here, :]
+        bq, bv = vecs_ref[2:3, :], vecs_ref[3:4, :]
+        q = mm(a1, attn_w[0].reshape(width, width))
+        qkv_ref[here, 0:width] = ((q + bq) * 0.125).astype(BF16)
+        k = mm(a1, attn_w[1].reshape(width, width))
+        qkv_ref[here, width : 2 * width] = k.astype(BF16)
+        v = mm(a1, attn_w[2].reshape(width, width))
+        qkv_ref[here, 2 * width : 3 * width] = (v + bv).astype(BF16)
+
+    def between_heads(head):
+        for pair in range(6):
+            if 4 + 2 * pair + head in slots_of or 4 + 2 * pair + head == 15:
+                @pl.when(pid == 5 + pair)
+                def _():
+                    between(4 + 2 * pair + head)
+
+    @pl.when(pid >= 5)
+    def _():
+        cols = [pl.ds(pl.multiple_of(p * width + (pid - 5) * 128, 128), 128) for p in range(3)]
+        attn_fwd_kernel(
+            qkv_ref.at[:, cols[0]], qkv_ref.at[:, cols[1]], qkv_ref.at[:, cols[2]], kbias_ref, rbias_ref,
+            o_ref, qa_ref, mask_ref, between=between_heads,
+        )
+
+    @pl.when(pid == 10)
+    def _():
+        between(16)
+        mates_done(2 * nz - 2, len(units))
+        own_copies()[2].wait_recv()
+        own_keeps()[2].wait()
+        outward(2).start()
+        for g in range(3):
+            outward(g).wait()
+        for u in range(len(units)):
+            fetch(u).wait_send()
+            for made in stage_one(u) + stage_two(u) + [stage_three(u)]:
+                made.wait_send()
+        for made in own_copies() + small_copies():
+            made.wait_send()
+
+
+SLOTS = {1: (0,), 3: (1,), 5: (2,), 7: (3,), 9: (4,), 11: (5,), 13: (6,), 15: (7,)}
+
+
+def head_forward(w_qkv, w_out, w_up, w_down, small, x, cells, lengths, nz):
+    rows, width = x.shape
+    r = w_qkv.shape[0]
+    copies = 3 * (nz - 1) * 9 + 3 + 2 * nz - 1
+    any_spec = pl.BlockSpec(memory_space=pl.ANY)
+    events = 2 * (nz - 1) + 2
+    slots_of = SLOTS if nz == 4 else {}
+    if not slots_of:
+        for t in range(events):
+            slots_of.setdefault(t * 16 // events, []).append(t)
+
+    def shape(*s, t=BF16):
+        return jax.ShapeDtypeStruct(s, t)
+
+    return pl.pallas_call(
+        partial(head_kernel, nz, slots_of),
+        grid=(11,),
+        in_specs=[any_spec] * 4 + [
+            whole(small.shape), whole(x.shape), whole(cells.shape), pl.BlockSpec(memory_space=pltpu.SMEM),
+        ],
+        out_specs=[
+            any_spec, any_spec, whole((16, width)), whole((1, 4 * width)), whole((rows, 128)),
+            whole((rows, width)), whole((rows, 3 * width)),
+            pl.BlockSpec((rows, 128), lambda i: (0, jnp.maximum(i - 5, 0))),
+            pl.BlockSpec((rows, 256), lambda i: (0, jnp.maximum(i - 5, 0))),
+        ],
+        out_shape=[
+            shape(8, 2 * nz, r, width), shape(2 * nz, 4, r, width), shape(16, width, t=F32),
+            shape(1, 4 * width, t=F32), shape(rows, 128), shape(rows, width), shape(rows, 3 * width),
+            shape(rows, width), shape(rows, 2 * width),
+        ],
+        scratch_shapes=[
+            pltpu.VMEM((12, r, width), BF16),
+            pltpu.VMEM((4, 2 * nz, r, width), BF16),
+            pltpu.VMEM((4, 2 * nz, r, width), BF16),
+            pltpu.VMEM((2 * nz, 4, r, width), BF16),
+            pltpu.VMEM((1, rows), F32),
+            pltpu.VMEM((2 * nz, 16, 128), BF16),
+            pltpu.VMEM((rows // TILE, TILE, TILE), F32),
+            pltpu.SemaphoreType.DMA((copies,)),
+            pltpu.SemaphoreType.DMA((copies,)),
+            pltpu.SemaphoreType.DMA((18,)),
+        ],
+        compiler_params=params(collective_id=0, has_side_effects=True),
+        cost_estimate=cost(6 * rows * width * width + 8 * rows * rows * width, 24 * rows * width),
+        name="head_forward",
+    )(w_qkv, w_out, w_up, w_down, small, x, cells, lengths)
+
+
 def core_split(res_ref, core, r, nz, send_ref, keep_ref):
     for i in range(nz):
         base = i * 2 * r
@@ -566,8 +797,12 @@
         keep_ref[0, i] = res_ref[pl.ds(pl.multiple_of(base + core * r, 8), r), :].astype(BF16)
 
 
-def grad_up_kernel(nz, r, ids_ref, a_ref, b_ref, send_ref, keep_ref, res_ref):
-    res_ref[...] = mm_tn(a_ref[...], b_ref[...])
+def grad_up_kernel(nz, r, ids_ref, a_ref, b_ref, send_ref, keep_ref, res_ref, at_ref):
+    @pl.when(pl.program_id(0) == 0)
+    def _():
+        at_ref[...] = a_ref[...].T
+
+    res_ref[...] = mm(at_ref[...], b_ref[...])
     core_split(res_ref, ids_ref[2], r, nz, send_ref, keep_ref)
 
 
@@ -587,44 +822,13 @@
                 pl.BlockSpec((rows, m), lambda i, ids: (0, i)),
             ],
             out_specs=[out, out],
-            scratch_shapes=[pltpu.VMEM((m, m), F32)],
+            scratch_shapes=[pltpu.VMEM((m, m), F32), pltpu.VMEM((m, rows), BF16)],
         ),
         out_shape=[half, half],
         compiler_params=params(),
         cost_estimate=cost(2 * rows * m * b.shape[1], 2 * (rows * m + rows * b.shape[1] + m * b.shape[1])),
         name="grad_up",
     )(ids, a, b)
-
-
-def grad_attn_kernel(nz, r, ids_ref, a_ref, o_ref, q_ref, k_ref, v_ref, y_ref, send_ref, keep_ref, res_ref):
-    step = pl.program_id(0)
-    for i, (left, right) in enumerate(((a_ref, q_ref), (a_ref, k_ref), (a_ref, v_ref), (o_ref, y_ref))):
-        @pl.when(step == i)
-        def _():
-            res_ref[...] = mm_tn(left[...], right[...])
-    core_split(res_ref, ids_ref[2], r, nz, send_ref, keep_ref)
-
-
-def grad_attn_split(ids, a1, o, dq, dk, dv, dy, nz):
-    rows, m = a1.shape
-    r = m // (2 * nz)
-    half = jax.ShapeDtypeStruct((4, nz, r, m), BF16)
-    out = pl.BlockSpec((1, nz, r, m), lambda i, ids: (i, 0, 0, 0))
-    full = pl.BlockSpec((rows, m), lambda i, ids: (0, 0), pipeline_mode=pl.Buffered(1))
-    return pl.pallas_call(
-        partial(grad_attn_kernel, nz, r),
-        grid_spec=pltpu.PrefetchScalarGridSpec(
-            num_scalar_prefetch=1,
-            grid=(4,),
-            in_specs=[full] * 6,
-            out_specs=[out, out],
-            scratch_shapes=[pltpu.VMEM((m, m), F32)],
-        ),
-        out_shape=[half, half],
-        compiler_params=params(),
-        cost_estimate=cost(8 * rows * m * m, 2 * (6 * rows * m + 4 * m * m)),
-        name="grad_attn",
-    )(ids, a1, o, dq, dk, dv, dy)
 
 
 def grad_down_kernel(r, ids_ref, a_ref, b_ref, send_ref, keep_ref, res_ref):
@@ -666,13 +870,15 @@
 
 
 class Exchange:
-    def __init__(self, sends, keeps, mine, core_in, x_in, y_in, x2_in, y2_in, z_in, owned, dp_in, sems):
+    def __init__(self, sends, keeps, late, mine, core_in, x_in, y_in, x2_in, y2_in, z_in, owned, dp_in, sems):
         self.sends, self.keeps = sends, keeps
         self.mine, self.core_in = mine, core_in
         self.x_in, self.y_in, self.x2_in, self.y2_in = x_in, y_in, x2_in, y2_in
         self.z_in, self.owned, self.dp_in = z_in, owned, dp_in
         self.send_sem, self.recv_sem, self.load_sem = sems
-        self.groups = len(sends)
+        self.groups = len(sends) + 1
+        self.late = late
+        self.early = len(sends)
         self.nz = mine.shape[0] // self.groups
         self.half = mine.shape[3] // 2
         self.units = self.groups * self.nz
@@ -701,6 +907,13 @@
     def owner(self, u):
         return lax.rem(self.z + 1 + u % self.nz, self.nz)
 
+    def late_copy(self, block):
+        first = self.units - self.nz
+        return self.remote(
+            self.late.at[block], self.core_in.at[pl.ds(first, self.nz), block], (first + block) * 8,
+            (self.d, self.mate),
+        )
+
     def core_copy(self, u):
         src = self.sends[u // self.nz].at[:, self.owner(u)]
         return self.remote(src, self.core_in.at[u], u * 8, (self.d, self.mate))
@@ -742,9 +955,9 @@
         ]
 
     def start(self):
-        for u in range(self.units):
+        for u in range(AHEAD):
             self.core_copy(u).start()
-        for u in range(self.units):
+        for u in range(self.units - self.nz):
             self.load(u).start()
 
     def add(self, u, block, cols, term):
@@ -752,8 +965,14 @@
         self.mine[u, block, :, cols] = value.astype(BF16)
 
     def stage_one(self, u):
-        self.load(u).wait()
-        self.core_copy(u).wait_recv()
+        if u < self.units - self.nz:
+            self.load(u).wait()
+            self.core_copy(u).wait_recv()
+            if u + AHEAD < self.units - self.nz:
+                self.core_copy(u + AHEAD).start()
+        elif u == self.units - self.nz:
+            for block in range(4):
+                self.late_copy(block).wait_recv()
         for block in range(4):
             self.add(u, block, slice(None), self.core_in[u, block])
         for made in self.plane_copies(u):
@@ -801,25 +1020,37 @@
 
     def finish(self):
         for u in range(self.units):
-            self.core_copy(u).wait_send()
+            if u < self.units - self.nz:
+                self.core_copy(u).wait_send()
             for made in self.plane_copies(u) + self.second_copies(u):
                 made.wait_send()
             if u % self.nz != self.nz - 1:
                 self.owner_copy(u).wait_send()
+        for block in range(4):
+            self.late_copy(block).wait_send()
         for g in range(self.groups):
             for made in self.dp_copies(g):
                 made.wait_send()
 
     def steps(self):
-        return self.units + 2
+        return self.units + LAG_THREE
 
     def step(self, t):
         if t < self.units:
             self.stage_one(t)
-        if 1 <= t <= self.units:
-            self.stage_two(t - 1)
-        if 2 <= t:
-            self.stage_three(t - 2)
+        if LAG_TWO <= t < self.units + LAG_TWO:
+            self.stage_two(t - LAG_TWO)
+        if LAG_THREE <= t:
+            self.stage_three(t - LAG_THREE)
+        for g in range(self.groups - 1):
+            if t == (g + 1) * self.nz - 1 + LAG_FOUR:
+                self.stage_four(g)
+
+
+AHEAD = 2
+LAG_TWO = 1
+LAG_THREE = 2
+LAG_FOUR = 4
 
 
 def exchange_scratch(groups, nz, r, width, extra=0):
@@ -842,93 +1073,29 @@
     ]
 
 
-def attn_bwd_exchange_kernel(
-    qa_ref, k_ref, v_ref, o_ref, do_ref, kbias_ref, up_send, up_keep, down_send, down_keep,
-    dq_ref, dk_ref, dv_ref, up_ref, down_ref, mask_ref, doa_ref, dqt_ref, *scratch,
+def backward_kernel(
+    qa_ref, k_ref, v_ref, o_ref, do_ref, kbias_ref, a1_ref, of_ref, dy_ref, x_ref, dr_ref, w_ref, vec_ref,
+    s_bo_ref, s_g2_ref, s_h2_ref, s_bd_ref, s_bu_ref, up_send, up_keep, down_send, down_keep,
+    out_ref, up_ref, down_ref, qkv_ref, wo_ref, sums_ref,
+    mask_ref, doa_ref, dqt_ref, dq_ref, dk_ref, dv_ref, a1t_ref, res_ref, late_ref, small_in, *scratch,
 ):
-    ex = Exchange((down_send, up_send), (down_keep, up_keep), *scratch[:9], scratch[9:])
+    ex = Exchange((down_send, up_send), (down_keep, up_keep), late_ref, *scratch[:9], scratch[9:])
     pid = pl.program_id(0)
-    grid = 6
-    slots = 2 * grid - 1
-
-    @pl.when(pid == 0)
-    def _():
-        ex.barrier()
-        ex.start()
+    width = x_ref.shape[1]
+    nz = ex.nz
+    r = late_ref.shape[2]
+    heads, tiles = 6, 4
+    last_slot = 2 * heads + 4 + tiles
 
     plan = {}
-    total = ex.steps()
-    for t in range(total):
-        plan.setdefault(1 + t * min(slots, total) // total, []).append(t)
-
-    def between(half):
-        for slot, todo in plan.items():
-            if slot % 2 == half:
-                @pl.when(pid == slot // 2)
-                def _():
-                    for t in todo:
-                        ex.step(t)
-
-    attn_bwd_kernel(
-        qa_ref, k_ref, v_ref, o_ref, do_ref, kbias_ref, dq_ref, dk_ref, dv_ref, mask_ref, doa_ref, dqt_ref,
-        between=between,
-    )
-
-    @pl.when(pid == grid - 1)
-    def _():
-        r = down_send.shape[2]
-        width = down_send.shape[3]
-        ex.stage_four(0)
-        ex.stage_four(1)
-        for block, value in ex.blocks(0):
-            down_ref[pl.ds(pl.multiple_of(block * r, 8), r), :] = value
-        for block, value in ex.blocks(1):
-            up_ref[:, pl.ds(pl.multiple_of(block * width, 128), width)] = value
-        ex.finish()
-
-
-def attn_backward_exchange(qa, qkv, o, do, kbias, up_halves, down_halves, nz):
-    rows, width = o.shape
-    pairs = width // 128
-    r = up_halves[0].shape[2]
-
-    def part(p):
-        return pl.BlockSpec((rows, 128), lambda i: (0, p * pairs + i))
-
-    any_spec = pl.BlockSpec(memory_space=pl.ANY)
-    out = pl.BlockSpec((rows, 128), lambda i: (0, i))
-    shape = jax.ShapeDtypeStruct((rows, width), BF16)
-    return pl.pallas_call(
-        attn_bwd_exchange_kernel,
-        grid=(pairs,),
-        in_specs=[
-            pl.BlockSpec((rows, 256), lambda i: (0, i)), part(1), part(2), part(0), part(0),
-            whole(kbias.shape), any_spec, any_spec, any_spec, any_spec,
-        ],
-        out_specs=[out, out, out, whole((r, 4 * width)), whole((4 * r, width))],
-        out_shape=[
-            shape, shape, shape,
-            jax.ShapeDtypeStruct((r, 4 * width), F32), jax.ShapeDtypeStruct((4 * r, width), F32),
-        ],
-        scratch_shapes=[
-            pltpu.VMEM((rows // TILE, TILE, TILE), F32),
-            pltpu.VMEM((rows, 128), BF16),
-            pltpu.VMEM((128, rows), F32),
-        ] + exchange_scratch(2, nz, r, width),
-        compiler_params=params(collective_id=1, has_side_effects=True),
-        cost_estimate=cost(20 * rows * rows * width, 18 * rows * width),
-        name="attn_backward_exchange",
-    )(qa, qkv, qkv, o, do, kbias, *up_halves, *down_halves)
-
-
-def input_exchange_kernel(
-    x_ref, dq_ref, dk_ref, dv_ref, dr_ref, w_ref, vec_ref, s_bo_ref, s_g2_ref, s_h2_ref, s_bd_ref, s_bu_ref,
-    send_ref, keep_ref, out_ref, qkv_ref, wo_ref, sums_ref, small_in, *scratch,
-):
-    ex = Exchange((send_ref,), (keep_ref,), *scratch[:9], scratch[9:])
-    pid = pl.program_id(0)
-    steps = 4
-    width = x_ref.shape[1]
+    for t in range(ex.steps()):
+        early = t * (2 * heads + 4) // (2 * nz)
+        late = 2 * heads + 4 + (t - 2 * nz) * 8 // nz
+        plan.setdefault(min(last_slot, early if t < 2 * nz else late), []).append(t)
+
+    def at_slot(slot):
+        for t in plan.get(slot, ()):
+            ex.step(t)
 
     @pl.when(pid == 0)
     def _():
@@ -940,45 +1107,97 @@
         for i in range(4):
             sums_ref[8 + i : 9 + i, :] = s_bu_ref[:, i * width : (i + 1) * width]
 
-    xhat, inv_std = norm_forward(x_ref[...].astype(F32))
-    da = mm_nt(dq_ref[...], w_ref[0])
-    da += mm_nt(dk_ref[...], w_ref[1])
-    da += mm_nt(dv_ref[...], w_ref[2])
-    totals = (da * xhat, da, dq_ref[...].astype(F32), dv_ref[...].astype(F32))
-    for i, value in enumerate(totals):
-        sums_ref[i : i + 1, :] += jnp.sum(value, axis=0, keepdims=True)
-    out_ref[...] = dr_ref[...] + norm_backward(da, xhat, inv_std, vec_ref[0:1, :])
-
-    total = ex.steps()
-    for slot in range(steps):
-        todo = [t for t in range(total) if min(t * steps // ex.units, steps - 1) == slot]
-
-        @pl.when(pid == slot)
+    def between(half):
+        for step in range(heads):
+            if 2 * step + half in plan:
+                @pl.when(pid == step)
+                def _():
+                    at_slot(2 * step + half)
+
+    @pl.when(pid < heads)
+    def _():
+        cols = pl.ds(pl.multiple_of(pid * 128, 128), 128)
+        attn_bwd_kernel(
+            qa_ref, k_ref, v_ref, o_ref, do_ref, kbias_ref, dq_ref.at[:, cols], dk_ref.at[:, cols],
+            dv_ref.at[:, cols], mask_ref, doa_ref, dqt_ref, between=between,
+        )
+
+    first = ex.units - nz
+    for block, right in enumerate((dq_ref, dk_ref, dv_ref, dy_ref)):
+        @pl.when(pid == heads + block)
         def _():
-            for t in todo:
-                ex.step(t)
-
-    @pl.when(pid == steps - 1)
+            at_slot(2 * heads + block)
+            if block == 0:
+                a1t_ref[...] = a1_ref[...].T
+            if block < 3:
+                res_ref[...] = mm(a1t_ref[...], right[...])
+            else:
+                res_ref[...] = mm_tn(of_ref[...], right[...])
+            for j in range(nz):
+                base = ex.owner(j) * (2 * r)
+                there = pl.multiple_of(base + (1 - ex.c) * r, 8)
+                here = pl.multiple_of(base + ex.c * r, 8)
+                late_ref[block, j] = res_ref[pl.ds(there, r), :].astype(BF16)
+                ex.mine[first + j, block] = res_ref[pl.ds(here, r), :].astype(BF16)
+            ex.late_copy(block).start()
+
+    for tile in range(tiles):
+        @pl.when(pid == heads + 4 + tile)
+        def _():
+            at_slot(2 * heads + 4 + tile)
+
+    @pl.when(pid >= heads + 4)
     def _():
-        base = ex.units * 8 + 3
+        size = x_ref.shape[0]
+        here = pl.ds(pl.multiple_of((pid - heads - 4) * size, size), size)
+        xhat, inv_std = norm_forward(x_ref[...].astype(F32))
+        dq, dk, dv = dq_ref[here, :], dk_ref[here, :], dv_ref[here, :]
+        da = mm_nt(dq, w_ref[0])
+        da += mm_nt(dk, w_ref[1])
+        da += mm_nt(dv, w_ref[2])
+        for i, value in enumerate((da * xhat, da, dq.astype(F32), dv.astype(F32))):
+            sums_ref[i : i + 1, :] += jnp.sum(value, axis=0, keepdims=True)
+        out_ref[...] = dr_ref[...] + norm_backward(da, xhat, inv_std, vec_ref[0:1, :])
+
+    @pl.when(pid == heads + 4 + tiles - 1)
+    def _():
+        base = ex.units * 8 + 3 * ex.groups
         hops = [(ex.d, ex.mate), (ex.x, ex.f), (ex.y, ex.f)]
         small = []
 
-        def begin(i, device):
+        def begin(device):
+            i = len(small)
             made = ex.remote(sums_ref, small_in.at[i], base + i, device)
             made.start()
             small.append(made)
 
-        begin(0, hops[0])
-        ex.stage_four(0)
-        for i in range(3):
-            small[i].wait()
-            sums_ref[...] += small_in[i]
-            if i < 2:
-                begin(i + 1, hops[i + 1])
-        for k in range(1, ex.nz):
-            begin(2 + k, (ex.d, lax.rem(ex.z + k, ex.nz) * 2 + ex.c))
+        def end():
+            made = small[-1]
+            made.wait()
+            sums_ref[...] += small_in[len(small) - 1]
+
+        todo = list(plan.get(last_slot, ()))
+        begin(hops[0])
+        for i, t in enumerate(todo):
+            ex.step(t)
+            if i < 3:
+                end()
+                if i < 2:
+                    begin(hops[i + 1])
+        for k in range(1, nz):
+            begin((ex.d, lax.rem(ex.z + k, nz) * 2 + ex.c))
+        ex.stage_four(2)
         for block, value in ex.blocks(0):
+            down_ref[pl.ds(pl.multiple_of(block * r, 8), r), :] = value
+        for block, value in ex.blocks(1):
+            up_ref[:, pl.ds(pl.multiple_of(block * width, 128), width)] = value
+        for made in small[3:]:
+            made.wait()
+        total_small = sums_ref[...]
+        for k in range(1, nz):
+            total_small = total_small + small_in[2 + k]
+        sums_ref[...] = total_small
+        for block, value in ex.blocks(2):
             @pl.when(block < 3)
             def _():
                 qkv_ref[:, pl.ds(pl.multiple_of(block * width, 128), width)] = value
@@ -986,36 +1205,56 @@
             @pl.when(block == 3)
             def _():
                 wo_ref[...] = value
-        for made in small[3:]:
-            made.wait()
-        total_small = sums_ref[...]
-        for k in range(1, ex.nz):
-            total_small = total_small + small_in[2 + k]
-        sums_ref[...] = total_small
         ex.finish()
 
 
-def input_grad_exchange(x, dq, dk, dv, dr, ab, vecs, smalls, halves, nz):
-    rows, width = x.shape
+def backward(qa, qkv, o, do, kbias, a1, dy, x, dr, ab, vecs, smalls, up_halves, down_halves, nz):
+    rows, width = o.shape
+    pairs = width // 128
+    r = up_halves[0].shape[2]
     tile = rows // 4
-    r = halves[0].shape[2]
-    row = rows_spec(tile, width)
+
+    def part(p):
+        return pl.BlockSpec((rows, 128), lambda i: (0, p * pairs + jnp.minimum(i, pairs - 1)))
+
+    def row():
+        return pl.BlockSpec((tile, width), lambda i: (jnp.maximum(i - pairs - 4, 0), 0))
+
+    def f32(*shape):
+        return jax.ShapeDtypeStruct(shape, F32)
+
     any_spec = pl.BlockSpec(memory_space=pl.ANY)
     return pl.pallas_call(
-        input_exchange_kernel,
-        grid=(4,),
-        in_specs=[row, row, row, row, row, whole((3, width, width)), whole(vecs.shape)]
-        + [whole(s.shape) for s in smalls] + [any_spec, any_spec],
-        out_specs=[row, whole((r, 3 * width)), whole((r, width)), whole((16, width))],
+        backward_kernel,
+        grid=(pairs + 8,),
+        in_specs=[
+            pl.BlockSpec((rows, 256), lambda i: (0, jnp.minimum(i, pairs - 1))), part(1), part(2), part(0), part(0),
+            whole(kbias.shape), whole(a1.shape), whole(o.shape), whole(dy.shape), row(), row(),
+            whole((3, width, width)), whole(vecs.shape),
+        ] + [whole(s.shape) for s in smalls] + [any_spec] * 4,
+        out_specs=[
+            row(), whole((r, 4 * width)), whole((4 * r, width)), whole((r, 3 * width)), whole((r, width)),
+            whole((16, width)),
+        ],
         out_shape=[
-            jax.ShapeDtypeStruct((rows, width), F32), jax.ShapeDtypeStruct((r, 3 * width), F32),
-            jax.ShapeDtypeStruct((r, width), F32), jax.ShapeDtypeStruct((16, width), F32),
+            f32(rows, width), f32(r, 4 * width), f32(4 * r, width), f32(r, 3 * width), f32(r, width), f32(16, width),
         ],
-        scratch_shapes=[pltpu.VMEM((2 + nz, 16, width), F32)] + exchange_scratch(1, nz, r, width, 2 + nz),
-        compiler_params=params(collective_id=2, has_side_effects=True),
-        cost_estimate=cost(6 * rows * width * width, 16 * rows * width),
-        name="input_grad_exchange",
-    )(x, dq, dk, dv, dr, ab, vecs, *smalls, *halves)
+        scratch_shapes=[
+            pltpu.VMEM((rows // TILE, TILE, TILE), F32),
+            pltpu.VMEM((rows, 128), BF16),
+            pltpu.VMEM((128, rows), F32),
+            pltpu.VMEM((rows, width), BF16),
+            pltpu.VMEM((rows, width), BF16),
+            pltpu.VMEM((rows, width), BF16),
+            pltpu.VMEM((width, rows), BF16),
+            pltpu.VMEM((width, width), F32),
+            pltpu.VMEM((4, nz, r, width), BF16),
+            pltpu.VMEM((2 + nz, 16, width), F32),
+        ] + exchange_scratch(3, nz, r, width, 2 + nz),
+        compiler_params=params(collective_id=1, has_side_effects=True),
+        cost_estimate=cost(20 * rows * rows * width + 14 * rows * width * width, 40 * rows * width),
+        name="backward",
+    )(qa, qkv, qkv, o, do, kbias, a1, o, dy, x, dr, ab, vecs, *smalls, *up_halves, *down_halves)
 
 
 def per_device(
@@ -1028,37 +1267,38 @@
     nz = nf // 2
     f = lax.axis_index("fsdp")
     ids = jnp.stack([lax.axis_index("dp"), f // 2, f % 2]).astype(jnp.int32)
-    vectors = (ln1_gain, ln1_bias, b_query, b_value, b_out, ln2_gain, ln2_bias, b_down, b_up)
-    flat = jnp.concatenate(vectors)
-    small_rows = -(-flat.shape[0] // 2048) * 16
-    small = jnp.pad(flat, (0, small_rows * 128 - flat.shape[0])).reshape(small_rows, 128)
-    own = jnp.stack(
-        [w_qkv[:, i * width : (i + 1) * width] for i in range(3)]
-        + [w_out]
-        + [w_up[:, i * width : (i + 1) * width] for i in range(4)]
-        + [w_down[i * r : (i + 1) * r] for i in range(4)]
-    )
-    ab, down_full, smalls = gather_weights(own, small, nz)
-    ab = ab.reshape(8, width, width)
+    vectors = (ln1_gain, ln1_bias, b_query, b_value, b_out, ln2_gain, ln2_bias, b_down)
+    small = jnp.concatenate([v[None] for v in vectors] + [b_up.reshape(4, r)])
+    small = jnp.pad(small, ((0, 4), (0, 128 - r)))
+    x = tokens[0]
+    if r % 16 == 0:
+        ab, down_full, vecs, bu, kbias, a1, qkv, o, qa = head_forward(
+            w_qkv, w_out, w_up, w_down, small, x, cells, lengths, nz
+        )
+        ab = ab.reshape(8, width, width)
+    else:
+        own = jnp.stack(
+            [w_qkv[:, i * width : (i + 1) * width] for i in range(3)]
+            + [w_out]
+            + [w_up[:, i * width : (i + 1) * width] for i in range(4)]
+            + [w_down[i * r : (i + 1) * r] for i in range(4)]
+        )
+        ab, down_full, smalls = gather_weights(own, small, nz)
+        ab = ab.reshape(8, width, width)
+        smalls = smalls[:, :, :r].astype(F32)
+        vecs = smalls.transpose(1, 0, 2).reshape(16, width)
+        bu = smalls[:, 8:12].reshape(1, 4 * width)
+        kbias, rbias = mask_terms(lengths, cells, context)
+        a1, qkv = qkv_forward(x, ab, vecs, 0.125)
+        o, qa = attn_forward(qkv, kbias, rbias)
     down_full = down_full.reshape(4 * width, width)
-    smalls = smalls.reshape(nf, -1).astype(F32)
-    vecs = smalls[:, : 8 * r].reshape(nf, 8, r).transpose(1, 0, 2).reshape(8, width)
-    bu = smalls[:, 8 * r : 12 * r].reshape(1, 4 * width)
-    x = tokens[0]
-    kbias, rbias, valid = mask_terms(lengths, cells, context)
-    a1, qkv = qkv_forward(x, ab, vecs, 0.125)
-    o, qa = attn_forward(qkv, kbias, rbias)
     out, dm, a2, g, du, dr, dy, do, s_g2, s_h2, s_bu, s_bd, s_bo = mlp_both(
-        x, o, cotangent[0], valid, ab, down_full, vecs, bu
+        x, o, cotangent[0], lengths, ab, down_full, vecs, bu
     )
     down_halves = grad_down_split(ids, g, dm, nz)
     up_halves = grad_up_split(ids, a2, du, nz)
-    dq, dk, dv, grad_up, grad_down = attn_backward_exchange(
-        qa, qkv, o, do, kbias, up_halves, down_halves, nz
-    )
-    attn_halves = grad_attn_split(ids, a1, o, dq, dk, dv, dy, nz)
-    grad_x, grad_qkv, grad_out, sums = input_grad_exchange(
-        x, dq, dk, dv, dr, ab, vecs, (s_bo, s_g2, s_h2, s_bd, s_bu), attn_halves, nz
+    grad_x, grad_up, grad_down, grad_qkv, grad_out, sums = backward(
+        qa, qkv, o, do, kbias, a1, dy, x, dr, ab, vecs, (s_bo, s_g2, s_h2, s_bd, s_bu), up_halves, down_halves, nz
     )
     mine = lax.dynamic_slice(sums, (0, f * r), (8, r))
     g_g1, g_h1, g_bq, g_bv, g_bo, g_g2, g_h2, g_bd = (mine[i] for i in range(8))

time: 321 us -> 256 us (0.80)
  Pallas kernels: 292 us -> 241 us
  local copies, waits for them, and re-layouts: 25.5 us -> 12.4 us
    pallas_call x6 -> x2, Pallas kernels: 237 us -> 185 us  [the longest x1 105 us: backward(): pl.pallas_call(backward_kernel, grid=(pairs + 8,), in_specs=[pl.BlockSpec...]
    unnamed x55 -> x13, local copies, waits for them, and re-layouts: 20 us -> 7.52 us
where the time goes in v1:
time: 256 us; the launch traced here: 255 us
  Pallas kernels  241 us (94%)
  local copies, waits for them, and re-layouts  12.4 us (5%)
    pallas_call x1, Pallas kernels, backward(): pl.pallas_call(backward_kernel, grid=(pairs + 8,), in_specs=[pl.BlockSpec...  105 us
    pallas_call x1, Pallas kernels, head_forward(): pl.pallas_call(partial(head_kernel, nz, slots_of), grid=(11,), in_specs=[...  79.6 us
    pallas_call x1, Pallas kernels, mlp_both(): pl.pallas_call(mlp_kernel, grid=(rows // TILE,), in_specs=[row, row, row,...  35.4 us
    pallas_call x1, Pallas kernels, grad_up_split(): pl.pallas_call(partial(grad_up_kernel, nz, r), grid_spec=pltpu.PrefetchSc...  10.4 us
    pallas_call x1, Pallas kernels, grad_down_split(): pl.pallas_call(partial(grad_down_kernel, r), grid_spec=pltpu.PrefetchScal...  10.2 us
    unnamed x13, local copies, waits for them, and re-layouts  7.52 us

profile of v1, /device:TPU:0, one launch (start us, length us, event | category | flops | bytes accessed | tf_op | source)
XLA Modules:
  0.0 255.2 jit_solution(7884746987030375587)
XLA Ops:
  0.6 0.8 reshape.42
  1.4 0.8 concatenate.3
  2.2 0.6 pad.4.small_ref
  3.5 79.6 %head_forward.1 = (bf16[8,8,96,768]{3,2,1,0:T(8,128)(2,1)}, bf16[8,4,96,768]{3,2,1,0:T(8,128)(2,1)}, f32[16,768]{1,0:T(8,128)}, f32[1,3072]{1,0:T(1,128)}, bf16[...) custom-call(bf16[96,2304]{1,0:T(8,128)(2,1)} %wqkv_ref.1, ...), custom_call_target="tpu_custom_call" | custom-call | flops 10066329600 | bytes 18874368 | tf_op jit(solution)/shard_map/head_forward/pallas_call | solution.py:758
  83.1 35.4 %mlp_both.1 = (bf16[1024,768]{1,0:T(8,128)(2,1)}, bf16[1024,768]{1,0:T(8,128)(2,1)}, bf16[1024,768]{1,0:T(8,128)(2,1)}, bf16[1024,3072]{1,0:T(8,128)(2,1)}, bf16...) custom-call(bf16[1024,768]{1,0:T(8,128)(2,1)} %bitcast.44, ...), custom_call_target="tpu_custom_call" | custom-call | flops 21743271936 | bytes 56623104 | tf_op jit(solution)/shard_map/mlp_both/pallas_call | solution.py:326
  118.5 0.6 pad_add_fusion.ids_ref
  119.1 10.4 %grad_up.1 = (bf16[4,4,96,768]{3,2,1,0:T(8,128)(2,1)}, bf16[4,4,96,768]{3,2,1,0:T(8,128)(2,1)}) custom-call(s32[3]{0:T(128)} %pad_add_fusion.ids_ref, bf16[1024,768]{1,0:T(8,128)(2,1)} %get-tuple-element.65.a_ref, bf16[1024,3072]{1,0:T(8,128)(2,1)} %get-tuple-element.66.b_ref), custom_call_target="tpu_custom_call" | custom-call | flops 4831838208 | bytes 12582912 | tf_op jit(solution)/shard_map/grad_up/pallas_call | solution.py:815
  129.6 10.2 %grad_down.1 = (bf16[4,4,96,768]{3,2,1,0:T(8,128)(2,1)}, bf16[4,4,96,768]{3,2,1,0:T(8,128)(2,1)}) custom-call(s32[3]{0:T(128)} %pad_add_fusion.ids_ref, bf16[1024,3072]{1,0:T(8,128)(2,1)} %get-tuple-element.69.a_ref, bf16[1024,768]{1,0:T(8,128)(2,1)} %get-tuple-element.70.b_ref), custom_call_target="tpu_custom_call" | custom-call | flops 4831838208 | bytes 12582912 | tf_op jit(solution)/shard_map/grad_down/pallas_call | solution.py:853
  139.8 105.1 %backward.1 = (f32[1024,768]{1,0:T(8,128)}, f32[96,3072]{1,0:T(8,128)}, f32[384,768]{1,0:T(8,128)}, f32[96,2304]{1,0:T(8,128)}, f32[96,768]{1,0:T(8,128)}, /*index=5*/f32[16,768]{1,0:T(8,128)}) custom-call(bf16[1024,1536]{1,0:T(8,128)(2,1)} %get-tuple-element.53.qa_ref, bf16[1024,2304]{1,0:T(8,128)(2,1)} %get-tuple-element.54.k_ref.v_ref, ...), custom_call_target="tpu_custom_call" | custom-call | flops 24561844224 | bytes 31457280 | tf_op jit(solution)/shard_map/backward/pallas_call | solution.py:1227
  244.9 0.8 constant_dynamic-slice_fusion
  245.7 0.5 slice_bitcast_fusion
  246.2 0.7 slice.34
  247.0 0.7 dynamic_slice.7
  247.6 0.0 copy-start.2
  247.6 0.0 copy-start.3
  247.6 3.9 %copy.38 = f32[1,1024,768]{2,1,0:T(8,128)} copy(f32[1,1024,768]{2,1,0:T(8,128)} %bitcast.33) | data formatting | bytes 6291456
  251.5 0.0 copy-done.2
  251.5 0.0 copy-start.1
  251.5 0.0 copy-start
  251.5 0.9 copy.39
  252.4 0.0 copy-done.3
  252.4 0.7 copy.40
  253.1 0.0 copy-done.1
  253.1 1.0 copy.41
  254.1 0.0 copy-done
  254.1 1.0 copy.42
  (1 shorter events, 0.0 us)
Async XLA Ops:
  247.6 3.9 %copy-start.2 = (f32[96,2304]{1,0:T(8,128)S(1)}, f32[96,2304]{1,0:T(8,128)}, u32[]{:S(2)}) copy-start(f32[96,2304]{1,0:T(8,128)} %get-tuple-element.106) | copy-start | bytes 2654212
  247.6 4.8 %copy-start.3 = (f32[96,768]{1,0:T(8,128)S(1)}, f32[96,768]{1,0:T(8,128)}, u32[]{:S(2)}) copy-start(f32[96,768]{1,0:T(8,128)} %get-tuple-element.109) | copy-start | bytes 884740
  251.5 1.6 copy-start.1
  251.5 2.6 %copy-start = (f32[384,768]{1,0:T(8,128)S(1)}, f32[384,768]{1,0:T(8,128)}, u32[]{:S(2)}) copy-start(f32[384,768]{1,0:T(8,128)} %get-tuple-element.115) | copy-start | bytes 3538948
